TPU v7x, 256 devices: a whole 4x4x8 slice. The times are simulated.
256 devices in a mesh: section: 16 (over y, x), row: 16 (over z, core).
Axes of the slice: x: 4, y: 4, z: 8, core: 2. Of those that a mesh axis runs over, the one named last changes fastest.
Arguments:
- omega: bfloat16 [8192, 16384], P('section', 'row'), may hold values from -0.25 to 0.25
- basis: bfloat16 [16384, 4096], P('row', 'section'), may hold values from -6 to 6
- vectors: bfloat16 [4, 16384], P(None, 'row'), may hold values from -6 to 6
Outputs:
- ortho: float32 [4, 16384], P(None, ('row', 'section'))
- coeffs: float32 [4, 4096], P(None, 'section')
All inputs are finite; a program needn't handle non-finite values.
Results may differ from a plain program's by a relative error of at most 0.0021.
Values may be sent and summed in bfloat16 or wider, within the bound.
A program may use at most 64 MiB of HBM per device.

v0:
```python
import jax
import jax.numpy as jnp
from jax import lax
from jax.sharding import Mesh
from jax.sharding import PartitionSpec as P

SECTION = ("section_0", "section_1")
ROW_SECTION = ("row", "section_0", "section_1")


def split_up(x, dim, peers):
    lengths = x.shape
    tiles = x.reshape(*lengths[:dim], peers, lengths[dim] // peers, *lengths[dim + 1 :])
    return jnp.moveaxis(tiles, dim, 0)


def summed_on_arrival(x, axis, dim):
    tiles = split_up(x, dim, lax.axis_size(axis))
    arrived = lax.all_to_all(tiles, axis, split_axis=0, concat_axis=0, tiled=True)
    return arrived.sum(axis=0)


def in_order(tiles, dim):
    tiles = jnp.moveaxis(tiles, 0, dim)
    lengths = tiles.shape
    return tiles.reshape(*lengths[:dim], lengths[dim] * lengths[dim + 1], *lengths[dim + 2 :])


def from_everyone(x, axis):
    peers = lax.axis_size(axis)
    return lax.all_to_all(jnp.broadcast_to(x[None], (peers, *x.shape)), axis, 0, 0, tiled=True)


def gather_directly(x, axis, dim):
    return in_order(from_everyone(x, axis), dim)


def gathered_total(x, axis):
    return lax.all_gather(x, axis).sum(0)


def taken_together(x, axis):
    everything = from_everyone(x, axis)
    return jnp.sum(everything, axis=0)


def from_behind(value, axis, steps):
    count = lax.axis_size(axis)
    initial, last = (max(0, -steps), min(count, count - steps))
    return lax.ppermute(value, axis, [(source, source + steps) for source in range(initial, last)])


def broadcast_by_axis(x, axes, root):
    x = jnp.where(lax.axis_index(axes) == root, x, jnp.zeros_like(x))
    for axis in axes:
        x = lax.psum(x, axis)
    return x


def lower_solve(factor, right):
    return lax.linalg.triangular_solve(factor, right, left_side=True, lower=True, transpose_a=False)


def factor_solve(factor, right):
    half = lower_solve(factor, right)
    return lax.linalg.triangular_solve(factor, half, left_side=True, lower=True, transpose_a=True)


def body(omega, basis, vectors):
    hi = lax.Precision.HIGHEST
    sections = lax.axis_size(SECTION)
    my_section = lax.axis_index(SECTION)
    every = lax.all_gather(basis, SECTION, axis=1, tiled=True)
    spread = lax.psum_scatter(
        jnp.dot(omega, every, preferred_element_type=jnp.float32),
        "row",
        scatter_dimension=0,
        tiled=True,
    )
    sketch = lax.all_to_all(spread, SECTION, split_axis=1, concat_axis=0, tiled=True)
    probe_term = lax.dot_general(
        vectors, omega, (((1,), (1,)), ((), ())), preferred_element_type=jnp.float32
    )
    piece = summed_on_arrival(probe_term, "row", 1)
    probe = gather_directly(piece, SECTION, 1)
    gram = gathered_total(jnp.dot(sketch.T, sketch, precision=hi), "row")
    factor = jnp.linalg.cholesky(gram)

    def project(current):
        inner = jnp.dot(current, sketch, precision=hi)
        inner = taken_together(inner, "row")
        coef = factor_solve(factor, inner.T).T
        return (coef, current - jnp.dot(coef, sketch.T, precision=hi))

    def advance(step, carry):
        current, kept = carry
        coef, moved = project(current)
        active = my_section == step
        kept = jnp.where(active, coef, kept)
        moved = jnp.where(active, moved, current)
        return (from_behind(moved, SECTION, 1), kept)

    start_coef = jnp.zeros((vectors.shape[0], basis.shape[1]), jnp.float32)
    probe, kept = lax.fori_loop(0, sections - 1, advance, (probe, start_coef))
    coef, moved = project(probe)
    finished = my_section == sections - 1
    kept = jnp.where(finished, coef, kept)
    final = broadcast_by_axis(moved, SECTION, sections - 1)
    rounded = kept.astype(jnp.bfloat16)
    own_term = lax.dot_general(
        rounded, basis, (((1,), (1,)), ((), ())), preferred_element_type=jnp.float32
    )
    removed = summed_on_arrival(own_term, SECTION, 1)
    width = removed.shape[1]
    mine = lax.dynamic_slice_in_dim(vectors, my_section * width, width, 1)
    remain = mine.astype(jnp.float32) - removed
    small = taken_together(jnp.dot(final, final.T, precision=hi), "row")
    lower = jnp.linalg.cholesky(small)
    ortho = lower_solve(lower, remain)
    return (ortho, kept)


def solution(mesh):
    finer = Mesh(mesh.devices.reshape(4, 4, mesh.shape["row"]), ("section_0", "section_1", "row"))
    placed = (P(SECTION, "row"), P("row", SECTION), P(None, "row"))
    return jax.shard_map(
        body,
        mesh=finer,
        in_specs=placed,
        out_specs=(P(None, ROW_SECTION), P(None, SECTION)),
        check_vma=False,
    )
```

profile of v0, /device:TPU:1, one launch (start us, length us, event | category | flops | bytes accessed | tf_op | source)
XLA Modules:
  0.0 975.5 jit_solution(7183521388998727887)
XLA Ops:
  8.0 87.1 %all-gather.4.cloned.1.call-done = bf16[1024,4096]{1,0:T(8,128)(2,1)} async-done(((bf16[1024,256]{1,0:T(8,128)(2,1)}), bf16[1024,4096]{1,0:T(8,128)(2,1)}) %all-gather.4.cloned.1.call-update) | async-done | bytes 8388624 | tf_op jit(solution)/shard_map/all_gather | solution.py:73
  95.1 10.0 %fusion.39 = f32[512,4096]{1,0:T(8,128)} fusion(bf16[512,1024]{1,0:T(8,128)(2,1)S(1)} %copy-done, bf16[1024,4096]{1,0:T(8,128)(2,1)} %all-gather.4.cloned.1.call-done), kind=kOutput, calls=%fused_computation.83 | convolution fusion | flops 4294967296 | bytes 17825792 | tf_op jit(solution)/shard_map/dot_general | solution.py:75
  105.2 68.9 %reduce-scatter.2.cloned.1.call-done = f32[32,4096]{1,0:T(8,128)} async-done(((f32[512,4096]{1,0:T(8,128)}), f32[32,4096]{1,0:T(8,128)}) %reduce-scatter.2.cloned.1.call-update) | async-done | bytes 524304 | tf_op jit(solution)/shard_map/reduce_scatter | solution.py:74
  175.1 15.6 %all_to_all.55 = f32[32,16,256]{2,0,1:T(8,128)S(1)} all-to-all(f32[32,16,256]{2,0,1:T(8,128)S(1)} %bitcast.147), channel_id=1, replica_groups=mesh['section_0'=4,'section_1'=4,'row'=16] {'section_0','section_1'}, dimensions={1} | all-to-all | bytes 1048576 | tf_op jit(solution)/shard_map/all_to_all | solution.py:80
  193.1 16.3 %all_to_all.56 = f32[16,1,128]{2,1,0:T(1,128)S(1)} all-to-all(f32[16,1,128]{2,1,0:T(1,128)S(1)} %reshape.114), channel_id=1, replica_groups=mesh['section_0'=4,'section_1'=4,'row'=16] {'row'}, dimensions={0} | all-to-all | bytes 16384 | tf_op jit(solution)/shard_map/all_to_all | solution.py:19
  215.2 6.0 all-to-all-done.2
  222.1 11.9 %all-gather.6.cloned.1.call-done = f32[4096,256]{1,0:T(8,128)} async-done(((f32[256,256]{1,0:T(8,128)}), f32[4096,256]{1,0:T(8,128)}) %all-gather.6.cloned.1.call-update) | async-done | bytes 4194320 | tf_op jit(solution)/shard_map/all_gather | solution.py:39
  236.7 11.7 %cholesky.64 = f32[128,128]{1,0:T(8,128)S(1)} custom-call(f32[128,128]{1,0:T(8,128)S(1)} %cholesky.153), custom_call_target="Cholesky" | custom-call | tf_op jit(solution)/shard_map/jit(cholesky)/cholesky | solution.py:87
  248.5 9.8 %custom-call.23 = f32[1,128,128]{1,2,0:T(8,128)S(1)} custom-call(f32[1,128,128]{2,1,0:T(8,128)S(1)} %get-tuple-element.206), custom_call_target="InvertDiagBlocksLowerTriangular" | custom-call | tf_op jit(solution)/shard_map/jit(cholesky)/cholesky | solution.py:87
  258.7 11.7 %cholesky.131 = f32[128,128]{1,0:T(8,128)S(1)} custom-call(f32[128,128]{1,0:T(8,128)S(1)} %convolution_subtract_fusion.3), custom_call_target="Cholesky" | custom-call | tf_op jit(solution)/shard_map/jit(cholesky)/cholesky | solution.py:87
  272.5 604.6 %while.26 = (s32[]{:T(128)}, f32[4,512]{1,0:T(4,128)S(1)}, f32[4,256]{1,0:T(4,128)S(1)}, s32[]{:T(128)}, f32[512,256]{1,0:T(8,128)S(1)}, /*index=5*/f32[256,256]...) while((s32[]{:T(128)}, f32[4,512]{1,0:T(4,128)S(1)}, f32[4,256]{1,0:T(4,128)S(1)}, ...), condition=%wide.region_9.12_spmd.clone, body=%wide.region_7.0_spmd.clone.sunk | while | flops 17457160 | bytes 2539907 | solution.py:104
  273.7 4.5 all-to-all-start
  282.3 19.7 %custom-call.37 = f32[2,128,128]{1,2,0:T(8,128)S(1)} custom-call(f32[2,128,128]{2,1,0:T(8,128)S(1)} %get-tuple-element.303), custom_call_target="InvertDiagBlocksLowerTriangular" | custom-call | tf_op jit(solution)/shard_map/while/body/eval_jaxpr/triangular_solve/custom-call.4 | solution.py:66
  308.8 8.1 all-to-all-start
  317.0 3.9 while.28
  320.9 19.7 %custom-call.37 = f32[2,128,128]{1,2,0:T(8,128)S(1)} custom-call(f32[2,128,128]{2,1,0:T(8,128)S(1)} %get-tuple-element.303), custom_call_target="InvertDiagBlocksLowerTriangular" | custom-call | tf_op jit(solution)/shard_map/while/body/eval_jaxpr/triangular_solve/custom-call.4 | solution.py:66
  342.3 3.9 collective-permute-start
  348.0 8.1 all-to-all-start
  356.2 3.9 while.28
  360.1 19.7 %custom-call.37 = f32[2,128,128]{1,2,0:T(8,128)S(1)} custom-call(f32[2,128,128]{2,1,0:T(8,128)S(1)} %get-tuple-element.303), custom_call_target="InvertDiagBlocksLowerTriangular" | custom-call | tf_op jit(solution)/shard_map/while/body/eval_jaxpr/triangular_solve/custom-call.4 | solution.py:66
  381.5 3.9 collective-permute-start
  387.2 8.1 all-to-all-start
  399.3 19.7 %custom-call.37 = f32[2,128,128]{1,2,0:T(8,128)S(1)} custom-call(f32[2,128,128]{2,1,0:T(8,128)S(1)} %get-tuple-element.303), custom_call_target="InvertDiagBlocksLowerTriangular" | custom-call | tf_op jit(solution)/shard_map/while/body/eval_jaxpr/triangular_solve/custom-call.4 | solution.py:66
  420.7 3.9 collective-permute-start
  426.4 8.1 all-to-all-start
  438.5 19.7 %custom-call.37 = f32[2,128,128]{1,2,0:T(8,128)S(1)} custom-call(f32[2,128,128]{2,1,0:T(8,128)S(1)} %get-tuple-element.303), custom_call_target="InvertDiagBlocksLowerTriangular" | custom-call | tf_op jit(solution)/shard_map/while/body/eval_jaxpr/triangular_solve/custom-call.4 | solution.py:66
  459.9 3.9 collective-permute-start
  465.6 8.1 all-to-all-start
  477.7 19.7 %custom-call.37 = f32[2,128,128]{1,2,0:T(8,128)S(1)} custom-call(f32[2,128,128]{2,1,0:T(8,128)S(1)} %get-tuple-element.303), custom_call_target="InvertDiagBlocksLowerTriangular" | custom-call | tf_op jit(solution)/shard_map/while/body/eval_jaxpr/triangular_solve/custom-call.4 | solution.py:66
  499.1 5.4 collective-permute-start
  506.3 8.1 all-to-all-start
  518.4 19.7 %custom-call.37 = f32[2,128,128]{1,2,0:T(8,128)S(1)} custom-call(f32[2,128,128]{2,1,0:T(8,128)S(1)} %get-tuple-element.303), custom_call_target="InvertDiagBlocksLowerTriangular" | custom-call | tf_op jit(solution)/shard_map/while/body/eval_jaxpr/triangular_solve/custom-call.4 | solution.py:66
  539.8 6.0 collective-permute-start
  547.6 8.1 all-to-all-start
  559.7 19.7 %custom-call.37 = f32[2,128,128]{1,2,0:T(8,128)S(1)} custom-call(f32[2,128,128]{2,1,0:T(8,128)S(1)} %get-tuple-element.303), custom_call_target="InvertDiagBlocksLowerTriangular" | custom-call | tf_op jit(solution)/shard_map/while/body/eval_jaxpr/triangular_solve/custom-call.4 | solution.py:66
  581.2 6.0 collective-permute-start
  588.9 8.1 all-to-all-start
  601.0 19.7 %custom-call.37 = f32[2,128,128]{1,2,0:T(8,128)S(1)} custom-call(f32[2,128,128]{2,1,0:T(8,128)S(1)} %get-tuple-element.303), custom_call_target="InvertDiagBlocksLowerTriangular" | custom-call | tf_op jit(solution)/shard_map/while/body/eval_jaxpr/triangular_solve/custom-call.4 | solution.py:66
  622.5 6.0 collective-permute-start
  630.2 8.1 all-to-all-start
  642.3 19.7 %custom-call.37 = f32[2,128,128]{1,2,0:T(8,128)S(1)} custom-call(f32[2,128,128]{2,1,0:T(8,128)S(1)} %get-tuple-element.303), custom_call_target="InvertDiagBlocksLowerTriangular" | custom-call | tf_op jit(solution)/shard_map/while/body/eval_jaxpr/triangular_solve/custom-call.4 | solution.py:66
  663.8 6.0 collective-permute-start
  671.5 8.1 all-to-all-start
  683.7 19.7 %custom-call.37 = f32[2,128,128]{1,2,0:T(8,128)S(1)} custom-call(f32[2,128,128]{2,1,0:T(8,128)S(1)} %get-tuple-element.303), custom_call_target="InvertDiagBlocksLowerTriangular" | custom-call | tf_op jit(solution)/shard_map/while/body/eval_jaxpr/triangular_solve/custom-call.4 | solution.py:66
  705.1 6.0 collective-permute-start
  712.9 8.1 all-to-all-start
  725.0 19.7 %custom-call.37 = f32[2,128,128]{1,2,0:T(8,128)S(1)} custom-call(f32[2,128,128]{2,1,0:T(8,128)S(1)} %get-tuple-element.303), custom_call_target="InvertDiagBlocksLowerTriangular" | custom-call | tf_op jit(solution)/shard_map/while/body/eval_jaxpr/triangular_solve/custom-call.4 | solution.py:66
  746.4 6.0 collective-permute-start
  754.2 8.1 all-to-all-start
  766.3 19.7 %custom-call.37 = f32[2,128,128]{1,2,0:T(8,128)S(1)} custom-call(f32[2,128,128]{2,1,0:T(8,128)S(1)} %get-tuple-element.303), custom_call_target="InvertDiagBlocksLowerTriangular" | custom-call | tf_op jit(solution)/shard_map/while/body/eval_jaxpr/triangular_solve/custom-call.4 | solution.py:66
  787.7 6.0 collective-permute-start
  795.5 8.1 all-to-all-start
  807.6 19.7 %custom-call.37 = f32[2,128,128]{1,2,0:T(8,128)S(1)} custom-call(f32[2,128,128]{2,1,0:T(8,128)S(1)} %get-tuple-element.303), custom_call_target="InvertDiagBlocksLowerTriangular" | custom-call | tf_op jit(solution)/shard_map/while/body/eval_jaxpr/triangular_solve/custom-call.4 | solution.py:66
  829.0 6.0 collective-permute-start
  836.8 8.1 all-to-all-start
  848.9 19.7 %custom-call.37 = f32[2,128,128]{1,2,0:T(8,128)S(1)} custom-call(f32[2,128,128]{2,1,0:T(8,128)S(1)} %get-tuple-element.303), custom_call_target="InvertDiagBlocksLowerTriangular" | custom-call | tf_op jit(solution)/shard_map/while/body/eval_jaxpr/triangular_solve/custom-call.4 | solution.py:66
  870.3 6.0 collective-permute-start
  878.1 8.1 all-to-all-start.4
  890.2 19.7 %custom-call.31 = f32[2,128,128]{1,2,0:T(8,128)S(1)} custom-call(f32[2,128,128]{2,1,0:T(8,128)S(1)} %get-tuple-element.168), custom_call_target="InvertDiagBlocksLowerTriangular" | custom-call | tf_op jit(solution)/shard_map/triangular_solve/custom-call.4 | solution.py:66
  911.6 20.6 %psum.14 = f32[4,512]{1,0:T(4,128)S(1)} all-reduce(f32[4,512]{1,0:T(4,128)S(1)} %fusion.10), channel_id=1, replica_groups=mesh['section_0'=4,'section_1'=4,'row'=16] {'section_0'}, use_global_device_ids=true, to_apply=%region_11.14 | all-reduce | flops 2048 | bytes 16384 | tf_op jit(solution)/shard_map/psum | solution.py:56
  932.3 6.1 psum.15
  939.1 11.0 %all-to-all-start.5 = ((f32[16,4,4]{2,1,0:T(4,128)}), f32[16,4,4]{2,1,0:T(4,128)S(1)}, u32[]{:S(2)}, u32[]{:S(2)}) async-start(f32[16,4,4]{2,1,0:T(4,128)} %broadcast_in_dim.46), calls=%async_computation.6 | async-start | bytes 65536 | tf_op jit(solution)/shard_map/all_to_all | solution.py:31
  951.2 6.3 all-to-all-done.5
  963.2 4.2 all-to-all-done.6
  (443 shorter events, 200.0 us)
Async XLA Ops:
  7.2 87.9 %copy-start = (bf16[512,1024]{1,0:T(8,128)(2,1)S(1)}, bf16[512,1024]{1,0:T(8,128)(2,1)}, u32[]{:S(2)}) copy-start(bf16[512,1024]{1,0:T(8,128)(2,1)} %param.9) | copy-start | bytes 3145732
  7.2 87.9 %all-gather.4.cloned.1.call-start = ((), (), s32[]{:S(2)}) async-start(), calls=%async_computation.8 | async-start | bytes 8912896 | tf_op jit(solution)/shard_map/all_gather | solution.py:73
  7.9 166.1 %reduce-scatter.2.cloned.1.call-start = ((), (), s32[]{:S(2)}) async-start(), calls=%async_computation.9 | async-start | bytes 8912896 | tf_op jit(solution)/shard_map/reduce_scatter | solution.py:74
  105.1 87.4 %copy-start.3 = (bf16[4,1024]{1,0:T(4,128)(2,1)S(1)}, bf16[4,1024]{1,0:T(4,128)(2,1)}, u32[]{:S(2)}) copy-start(bf16[4,1024]{1,0:T(4,128)(2,1)} %param.11) | copy-start | bytes 24580
  105.1 128.9 %all-gather.6.cloned.1.call-start = ((), (), s32[]{:S(2)}) async-start(), calls=%async_computation.10 | async-start | bytes 4456448 | tf_op jit(solution)/shard_map/all_gather | solution.py:39
  211.5 9.6 all-to-all-start.2
  272.5 677.6 %copy-start.1 = (bf16[1024,256]{1,0:T(8,128)(2,1)S(1)}, bf16[1024,256]{1,0:T(8,128)(2,1)}, u32[]{:S(2)}) copy-start(bf16[1024,256]{1,0:T(8,128)(2,1)} %param.10) | copy-start | bytes 1572868
  273.7 28.2 %all-to-all-start = ((f32[16,4,256]{2,1,0:T(4,128)}), f32[16,4,256]{2,1,0:T(4,128)S(1)}, u32[]{:S(2)}, u32[]{:S(2)}) async-start(f32[16,4,256]{2,1,0:T(4,128)} %broadcast_in_dim.50), calls=%async_computation | async-start | bytes 131072 | tf_op jit(solution)/shard_map/while/body/eval_jaxpr/all_to_all | solution.py:31
  303.7 4.1 collective-permute-start
  308.8 31.8 %all-to-all-start = ((f32[16,4,256]{2,1,0:T(4,128)}), f32[16,4,256]{2,1,0:T(4,128)S(1)}, u32[]{:S(2)}, u32[]{:S(2)}) async-start(f32[16,4,256]{2,1,0:T(4,128)} %broadcast_in_dim.50), calls=%async_computation | async-start | bytes 131072 | tf_op jit(solution)/shard_map/while/body/eval_jaxpr/all_to_all | solution.py:31
  342.3 4.7 collective-permute-start
  348.0 31.8 %all-to-all-start = ((f32[16,4,256]{2,1,0:T(4,128)}), f32[16,4,256]{2,1,0:T(4,128)S(1)}, u32[]{:S(2)}, u32[]{:S(2)}) async-start(f32[16,4,256]{2,1,0:T(4,128)} %broadcast_in_dim.50), calls=%async_computation | async-start | bytes 131072 | tf_op jit(solution)/shard_map/while/body/eval_jaxpr/all_to_all | solution.py:31
  381.5 4.7 collective-permute-start
  387.2 31.8 %all-to-all-start = ((f32[16,4,256]{2,1,0:T(4,128)}), f32[16,4,256]{2,1,0:T(4,128)S(1)}, u32[]{:S(2)}, u32[]{:S(2)}) async-start(f32[16,4,256]{2,1,0:T(4,128)} %broadcast_in_dim.50), calls=%async_computation | async-start | bytes 131072 | tf_op jit(solution)/shard_map/while/body/eval_jaxpr/all_to_all | solution.py:31
  420.7 4.7 collective-permute-start
  426.4 31.8 %all-to-all-start = ((f32[16,4,256]{2,1,0:T(4,128)}), f32[16,4,256]{2,1,0:T(4,128)S(1)}, u32[]{:S(2)}, u32[]{:S(2)}) async-start(f32[16,4,256]{2,1,0:T(4,128)} %broadcast_in_dim.50), calls=%async_computation | async-start | bytes 131072 | tf_op jit(solution)/shard_map/while/body/eval_jaxpr/all_to_all | solution.py:31
  459.9 4.7 collective-permute-start
  465.6 31.8 %all-to-all-start = ((f32[16,4,256]{2,1,0:T(4,128)}), f32[16,4,256]{2,1,0:T(4,128)S(1)}, u32[]{:S(2)}, u32[]{:S(2)}) async-start(f32[16,4,256]{2,1,0:T(4,128)} %broadcast_in_dim.50), calls=%async_computation | async-start | bytes 131072 | tf_op jit(solution)/shard_map/while/body/eval_jaxpr/all_to_all | solution.py:31
  499.1 6.2 collective-permute-start
  506.3 31.8 %all-to-all-start = ((f32[16,4,256]{2,1,0:T(4,128)}), f32[16,4,256]{2,1,0:T(4,128)S(1)}, u32[]{:S(2)}, u32[]{:S(2)}) async-start(f32[16,4,256]{2,1,0:T(4,128)} %broadcast_in_dim.50), calls=%async_computation | async-start | bytes 131072 | tf_op jit(solution)/shard_map/while/body/eval_jaxpr/all_to_all | solution.py:31
  539.8 6.8 collective-permute-start
  547.6 31.8 %all-to-all-start = ((f32[16,4,256]{2,1,0:T(4,128)}), f32[16,4,256]{2,1,0:T(4,128)S(1)}, u32[]{:S(2)}, u32[]{:S(2)}) async-start(f32[16,4,256]{2,1,0:T(4,128)} %broadcast_in_dim.50), calls=%async_computation | async-start | bytes 131072 | tf_op jit(solution)/shard_map/while/body/eval_jaxpr/all_to_all | solution.py:31
  581.2 6.8 collective-permute-start
  588.9 31.8 %all-to-all-start = ((f32[16,4,256]{2,1,0:T(4,128)}), f32[16,4,256]{2,1,0:T(4,128)S(1)}, u32[]{:S(2)}, u32[]{:S(2)}) async-start(f32[16,4,256]{2,1,0:T(4,128)} %broadcast_in_dim.50), calls=%async_computation | async-start | bytes 131072 | tf_op jit(solution)/shard_map/while/body/eval_jaxpr/all_to_all | solution.py:31
  622.5 6.8 collective-permute-start
  630.2 31.8 %all-to-all-start = ((f32[16,4,256]{2,1,0:T(4,128)}), f32[16,4,256]{2,1,0:T(4,128)S(1)}, u32[]{:S(2)}, u32[]{:S(2)}) async-start(f32[16,4,256]{2,1,0:T(4,128)} %broadcast_in_dim.50), calls=%async_computation | async-start | bytes 131072 | tf_op jit(solution)/shard_map/while/body/eval_jaxpr/all_to_all | solution.py:31
  663.8 6.8 collective-permute-start
  671.5 31.8 %all-to-all-start = ((f32[16,4,256]{2,1,0:T(4,128)}), f32[16,4,256]{2,1,0:T(4,128)S(1)}, u32[]{:S(2)}, u32[]{:S(2)}) async-start(f32[16,4,256]{2,1,0:T(4,128)} %broadcast_in_dim.50), calls=%async_computation | async-start | bytes 131072 | tf_op jit(solution)/shard_map/while/body/eval_jaxpr/all_to_all | solution.py:31
  705.1 6.8 collective-permute-start
  712.9 31.8 %all-to-all-start = ((f32[16,4,256]{2,1,0:T(4,128)}), f32[16,4,256]{2,1,0:T(4,128)S(1)}, u32[]{:S(2)}, u32[]{:S(2)}) async-start(f32[16,4,256]{2,1,0:T(4,128)} %broadcast_in_dim.50), calls=%async_computation | async-start | bytes 131072 | tf_op jit(solution)/shard_map/while/body/eval_jaxpr/all_to_all | solution.py:31
  746.4 6.8 collective-permute-start
  754.2 31.8 %all-to-all-start = ((f32[16,4,256]{2,1,0:T(4,128)}), f32[16,4,256]{2,1,0:T(4,128)S(1)}, u32[]{:S(2)}, u32[]{:S(2)}) async-start(f32[16,4,256]{2,1,0:T(4,128)} %broadcast_in_dim.50), calls=%async_computation | async-start | bytes 131072 | tf_op jit(solution)/shard_map/while/body/eval_jaxpr/all_to_all | solution.py:31
  787.7 6.8 collective-permute-start
  795.5 31.8 %all-to-all-start = ((f32[16,4,256]{2,1,0:T(4,128)}), f32[16,4,256]{2,1,0:T(4,128)S(1)}, u32[]{:S(2)}, u32[]{:S(2)}) async-start(f32[16,4,256]{2,1,0:T(4,128)} %broadcast_in_dim.50), calls=%async_computation | async-start | bytes 131072 | tf_op jit(solution)/shard_map/while/body/eval_jaxpr/all_to_all | solution.py:31
  829.0 6.8 collective-permute-start
  836.8 31.8 %all-to-all-start = ((f32[16,4,256]{2,1,0:T(4,128)}), f32[16,4,256]{2,1,0:T(4,128)S(1)}, u32[]{:S(2)}, u32[]{:S(2)}) async-start(f32[16,4,256]{2,1,0:T(4,128)} %broadcast_in_dim.50), calls=%async_computation | async-start | bytes 131072 | tf_op jit(solution)/shard_map/while/body/eval_jaxpr/all_to_all | solution.py:31
  870.3 6.8 collective-permute-start
  878.1 31.8 %all-to-all-start.4 = ((f32[16,4,256]{2,1,0:T(4,128)}), f32[16,4,256]{2,1,0:T(4,128)S(1)}, u32[]{:S(2)}, u32[]{:S(2)}) async-start(f32[16,4,256]{2,1,0:T(4,128)} %broadcast_in_dim.44), calls=%async_computation.5 | async-start | bytes 131072 | tf_op jit(solution)/shard_map/all_to_all | solution.py:31
  911.6 57.4 %copy-start.2 = (f32[4,256]{1,0:T(4,128)}, f32[4,256]{1,0:T(4,128)S(1)}, u32[]{:S(2)}) copy-start(f32[4,256]{1,0:T(4,128)S(1)} %bitcast_select_fusion.1) | copy-start | bytes 12292
  939.1 18.4 %all-to-all-start.5 = ((f32[16,4,4]{2,1,0:T(4,128)}), f32[16,4,4]{2,1,0:T(4,128)S(1)}, u32[]{:S(2)}, u32[]{:S(2)}) async-start(f32[16,4,4]{2,1,0:T(4,128)} %broadcast_in_dim.46), calls=%async_computation.6 | async-start | bytes 65536 | tf_op jit(solution)/shard_map/all_to_all | solution.py:31
  957.5 9.9 %all-to-all-start.6 = ((f32[16,1,256]{2,1,0:T(1,128)}), f32[16,1,256]{2,1,0:T(1,128)S(1)}, u32[]{:S(2)}, u32[]{:S(2)}) async-start(f32[16,1,256]{2,1,0:T(1,128)} %reshape.118), calls=%async_computation.7 | async-start | bytes 32768 | tf_op jit(solution)/shard_map/all_to_all | solution.py:19
Sparse Core Ops, SparseCore 0:
  10.4 84.6 all-gather.3
  105.3 68.7 reduce-scatter.1
  192.6 41.3 all-gather.5
where the time goes:
time: 978 us; the launch traced here: 976 us
  other arithmetic  357 us (37%)
  starting transfers between devices  223 us (23%)
  waiting for transfers between devices  197 us (20%)
  local copies, waits for them, and re-layouts  78.8 us (8%)
  blocking collectives  58.7 us (6%)
  matrix products  45.1 us (5%)
  between operations  15.3 us (2%)
    another operation x64, other arithmetic, factor_solve(): lax.linalg.triangular_solve(factor, half, left_side=True, lower=True, tra...  315 us
    all_to_all x18, starting transfers between devices, from_everyone(): lax.all_to_all(jnp.broadcast_to(x[None], (peers, *x.shape)), axis, 0, 0,...  140 us
    all_gather x1, waiting for transfers between devices, body(): every = lax.all_gather(basis, SECTION, axis=1, tiled=True)  87.1 us
    ppermute x15, starting transfers between devices, from_behind(): lax.ppermute(value, axis, [(source, source + steps) for source in range(i...  78.7 us
    reduce_scatter x1, waiting for transfers between devices, body(): lax.psum_scatter(jnp.dot(omega, every, preferred_element_type=jnp.float32...  68.9 us
    another operation x112, local copies, waits for them, and re-layouts, factor_solve(): lax.linalg.triangular_solve(factor, half, left_side=True, lower=True, tra...  63.2 us
    another operation x6, other arithmetic, body(): factor = jnp.linalg.cholesky(gram)  34 us
    psum x2, blocking collectives, broadcast_by_axis(): x = lax.psum(x, axis)  26.7 us
  transfers between devices with their start and end apart: 37, of which 21 were waited for; matrix products, arithmetic and copies ran while one was open for 39% of the time, Pallas kernels for 0%

commit v1 on v0

v1 whole, which is shorter than its diff:
```python
import functools

import jax
import jax.numpy as jnp
from jax import lax
from jax.experimental import pallas as pl
from jax.experimental.pallas import tpu as pltpu
from jax.sharding import PartitionSpec as P

F32 = jnp.float32
BF16 = jnp.bfloat16
HI = lax.Precision.HIGHEST
MESH = pl.DeviceIdType.MESH


def split(x):
    hi = x.astype(BF16)
    return hi, (x - hi.astype(F32)).astype(BF16)


def dot3(a, b, dims):
    (ah, al), (bh, bl) = a, b

    def one(x, y):
        return lax.dot_general(x, y, (dims, ((), ())), preferred_element_type=F32)

    return one(ah, bh) + (one(al, bh) + one(ah, bl))


NN = ((1,), (0,))
NT = ((1,), (1,))
TN = ((0,), (0,))


def remote(src, dst, send, recv, section, row):
    return pltpu.make_async_remote_copy(
        src_ref=src,
        dst_ref=dst,
        send_sem=send,
        recv_sem=recv,
        device_id=(section, row),
        device_id_type=MESH,
    )


def gram_kernel(
    ns, nr, s_ref, gram_ref, next_ref, part, got, red, rs_send, rs_recv, ag_send, ag_recv, n_send, n_recv
):
    s, r = lax.axis_index("section"), lax.axis_index("row")
    rows = part.shape[0] // nr
    barrier = pltpu.get_barrier_semaphore()
    after, before = lax.rem(s + 1, ns), lax.rem(s + ns - 1, ns)
    for step in range(1, nr):
        pl.semaphore_signal(barrier, inc=1, device_id=(s, lax.rem(r + step, nr)), device_id_type=MESH)
    pl.semaphore_signal(barrier, inc=1, device_id=(after, r), device_id_type=MESH)
    pl.semaphore_signal(barrier, inc=1, device_id=(before, r), device_id_type=MESH)
    sp = split(s_ref[...])
    part[...] = dot3(sp, sp, TN)
    pl.semaphore_wait(barrier, nr + 1)
    shift = remote(s_ref, next_ref, n_send, n_recv, before, r)
    shift.start()
    scatter = []
    for step in range(1, nr):
        peer = lax.rem(r + step, nr)
        cp = remote(
            part.at[pl.ds(pl.multiple_of(peer * rows, rows), rows)],
            got.at[step],
            rs_send.at[step],
            rs_recv.at[step],
            s,
            peer,
        )
        cp.start()
        scatter.append(cp)
    for cp in scatter:
        cp.wait_recv()
    total = part[pl.ds(pl.multiple_of(r * rows, rows), rows), :]
    for step in range(1, nr):
        total = total + got[step]
    red[...] = total
    mine = pl.ds(pl.multiple_of(r * rows, rows), rows)
    gather = []
    for step in range(1, nr):
        peer = lax.rem(r + step, nr)
        cp = remote(red, gram_ref.at[mine], ag_send.at[step], ag_recv.at[step], s, peer)
        cp.start()
        gather.append(cp)
    gram_ref[mine, :] = total
    for step in range(1, nr):
        peer = lax.rem(r + nr - step, nr)
        theirs = pl.ds(pl.multiple_of(peer * rows, rows), rows)
        remote(red, gram_ref.at[theirs], ag_send.at[step], ag_recv.at[step], s, peer).wait_recv()
    for cp in scatter + gather:
        cp.wait_send()
    shift.wait()


def gram_call(sketch, ns, nr):
    n = sketch.shape[1]
    vm = pl.BlockSpec(memory_space=pltpu.VMEM)
    dma = pltpu.SemaphoreType.DMA
    return pl.pallas_call(
        functools.partial(gram_kernel, ns, nr),
        out_shape=(
            jax.ShapeDtypeStruct((n, n), F32),
            jax.ShapeDtypeStruct(sketch.shape, F32),
        ),
        in_specs=[vm],
        out_specs=(vm, vm),
        scratch_shapes=[
            pltpu.VMEM((n, n), F32),
            pltpu.VMEM((nr, n // nr, n), F32),
            pltpu.VMEM((n // nr, n), F32),
            dma((nr,)),
            dma((nr,)),
            dma((nr,)),
            dma((nr,)),
            dma,
            dma,
        ],
        compiler_params=pltpu.CompilerParams(collective_id=0, has_side_effects=True),
    )(sketch)


def packed(c):
    half = c.shape[1] // 2
    return jnp.concatenate([c[:4, :half], c[:4, half:]], axis=0)


def unpacked(c):
    wide = jnp.concatenate([c[:4], c[4:]], axis=1)
    return jnp.concatenate([wide, jnp.zeros_like(wide)], axis=0)


def chain_kernel(
    ns,
    nr,
    s_ref,
    next_ref,
    inv_ref,
    p0_ref,
    basis_ref,
    vec_ref,
    ortho_ref,
    coef_ref,
    cross,
    probe,
    moved,
    cout,
    cin,
    own,
    oin,
    sout,
    sin,
    bout,
    bin_,
    c_send,
    c_recv,
    p_send,
    p_recv,
    o_send,
    o_recv,
    s_send,
    s_recv,
    b_send,
    b_recv,
):
    s, r = lax.axis_index("section"), lax.axis_index("row")
    barrier = pltpu.get_barrier_semaphore()
    after, before = lax.rem(s + 1, ns), lax.rem(s + ns - 1, ns)
    for q in range(nr):
        for other in (after, before):
            pl.semaphore_signal(barrier, inc=1, device_id=(other, q), device_id_type=MESH)
    for step in range(1, nr):
        pl.semaphore_signal(barrier, inc=1, device_id=(s, lax.rem(r + step, nr)), device_id_type=MESH)
    for step in range(1, ns):
        pl.semaphore_signal(barrier, inc=1, device_id=(lax.rem(s + step, ns), r), device_id_type=MESH)

    sp = split(s_ref[...])
    nx = split(next_ref[...])
    iv = split(inv_ref[...])
    cross[...] = dot3(sp, nx, TN)
    pl.semaphore_wait(barrier, 3 * nr + ns - 2)

    @pl.when(s == 0)
    def _():
        p = p0_ref[...]
        probe[...] = p
        cout[...] = packed(dot3(split(p), sp, NN))
        copies = []
        for step in range(1, nr):
            peer = lax.rem(r + step, nr)
            cp = remote(cout, cin.at[r], c_send.at[step], c_recv.at[r], 0, peer)
            cp.start()
            copies.append(cp)
        cin[pl.ds(r, 1)] = cout[...][None]
        for cp in copies:
            cp.wait_send()
        for step in range(1, nr):
            peer = lax.rem(r + step, nr)
            remote(cout, cin.at[peer], c_send.at[step], c_recv.at[peer], 0, peer).wait_recv()

    @pl.when(s > 0)
    def _():
        remote(moved, probe, p_send, p_recv, before, r).wait_recv()

    p = probe[...]
    ahead = dot3(split(p), nx, NN)

    @pl.when(s > 0)
    def _():
        for q in range(nr):
            remote(cout, cin.at[q], c_send.at[q], c_recv.at[q], before, q).wait_recv()

    total = cin[0]
    for q in range(1, nr):
        total = total + cin[q]
    inner = unpacked(total)
    coef = dot3(split(inner), iv, NN)
    cs = split(coef)

    @pl.when(s < ns - 1)
    def _():
        cout[...] = packed(ahead - dot3(cs, split(cross[...]), NN))
        for q in range(nr):
            remote(cout, cin.at[r], c_send.at[q], c_recv.at[r], after, q).start()

    moved[...] = p - dot3(cs, sp, NT)

    @pl.when(s < ns - 1)
    def _():
        remote(moved, probe, p_send, p_recv, after, r).start()

    coef_ref[...] = coef[:4]
    term = lax.dot_general(coef.astype(BF16), basis_ref[...], (NT, ((), ())), preferred_element_type=F32)
    for k in range(ns // 2):
        own[k] = term[:, k * 128 : (k + 1) * 128]
    outs = []
    for step in range(1, ns):
        t = lax.rem(s + step, ns)
        cp = remote(own.at[lax.div(t, 2)], oin.at[s], o_send.at[step], o_recv.at[s], t, r)
        cp.start()
        outs.append(cp)
    oin[pl.ds(s, 1)] = own[pl.ds(lax.div(s, 2), 1)]

    @pl.when(s == ns - 1)
    def _():
        m = split(moved[...])
        sq = dot3(m, m, NT)
        sout[...] = jnp.concatenate([sq, jnp.zeros((8, 120), F32)], axis=1)
        copies = []
        for step in range(1, nr):
            peer = lax.rem(r + step, nr)
            cp = remote(sout, sin.at[r], s_send.at[step], s_recv.at[r], s, peer)
            cp.start()
            copies.append(cp)
        sin[pl.ds(r, 1)] = sout[...][None]
        for step in range(1, nr):
            peer = lax.rem(r + step, nr)
            remote(sout, sin.at[peer], s_send.at[step], s_recv.at[peer], s, peer).wait_recv()
        tot = sin[0]
        for q in range(1, nr):
            tot = tot + sin[q]
        bout[...] = tot
        bcs = []
        for t in range(ns - 1):
            cp = remote(bout, bin_, b_send.at[t], b_recv, t, r)
            cp.start()
            bcs.append(cp)
        for cp in copies + bcs:
            cp.wait_send()
        bin_[...] = tot

    for step in range(1, ns):
        t = lax.rem(s + step, ns)
        remote(own.at[0], oin.at[t], o_send.at[step], o_recv.at[t], t, r).wait_recv()
    removed = oin[0]
    for t in range(1, ns):
        removed = removed + oin[t]
    odd = lax.rem(s, 2) == 1
    removed = jnp.where(odd, removed[:4, 64:], removed[:4, :64])
    remain = vec_ref[...].astype(F32) - removed

    @pl.when(s < ns - 1)
    def _():
        remote(bout, bin_, b_send.at[0], b_recv, ns - 1, r).wait_recv()
        for q in range(nr):
            remote(cout, cin.at[q], c_send.at[q], c_recv.at[q], after, q).wait_send()
        remote(moved, probe, p_send, p_recv, after, r).wait_send()

    small = bin_[...]

    def at(i, k):
        return small[i : i + 1, k : k + 1]

    low = [[None] * 4 for _ in range(4)]
    rows = []
    for i in range(4):
        for k in range(i + 1):
            v = at(i, k)
            for m in range(k):
                v = v - low[i][m] * low[k][m]
            low[i][k] = jnp.sqrt(v) if i == k else v / low[k][k]
        x = remain[i : i + 1]
        for k in range(i):
            x = x - low[i][k] * rows[k]
        rows.append(x / low[i][i])
    ortho_ref[...] = jnp.concatenate(rows, axis=0)
    for cp in outs:
        cp.wait_send()


def chain_call(sketch, nxt, inv, probe, basis, mine, ns, nr):
    vm = pl.BlockSpec(memory_space=pltpu.VMEM)
    dma = pltpu.SemaphoreType.DMA
    k, n = sketch.shape
    return pl.pallas_call(
        functools.partial(chain_kernel, ns, nr),
        out_shape=(
            jax.ShapeDtypeStruct((4, mine.shape[1]), F32),
            jax.ShapeDtypeStruct((4, n), F32),
        ),
        in_specs=[vm] * 6,
        out_specs=(vm, vm),
        scratch_shapes=[
            pltpu.VMEM((n, n), F32),
            pltpu.VMEM((8, k), F32),
            pltpu.VMEM((8, k), F32),
            pltpu.VMEM((8, 128), F32),
            pltpu.VMEM((nr, 8, 128), F32),
            pltpu.VMEM((ns // 2, 8, 128), F32),
            pltpu.VMEM((ns, 8, 128), F32),
            pltpu.VMEM((8, 128), F32),
            pltpu.VMEM((nr, 8, 128), F32),
            pltpu.VMEM((8, 128), F32),
            pltpu.VMEM((8, 128), F32),
            dma((nr,)),
            dma((nr,)),
            dma,
            dma,
            dma((ns,)),
            dma((ns,)),
            dma((nr,)),
            dma((nr,)),
            dma((ns,)),
            dma,
        ],
        compiler_params=pltpu.CompilerParams(collective_id=1, has_side_effects=True),
    )(sketch, nxt, inv, probe, basis, mine)


def lower_solve(factor, right):
    return lax.linalg.triangular_solve(factor, right, left_side=True, lower=True, transpose_a=False)


def inverse(gram):
    factor = jnp.linalg.cholesky(gram)
    half = lower_solve(factor, jnp.eye(gram.shape[0], dtype=F32))
    return jnp.dot(half.T, half, precision=HI)


def body(omega, basis, vectors):
    ns, nr = lax.axis_size("section"), lax.axis_size("row")
    s = lax.axis_index("section")
    every = lax.all_gather(basis, "section", axis=1, tiled=True)
    spread = lax.psum_scatter(
        jnp.dot(omega, every, preferred_element_type=F32), "row", scatter_dimension=0, tiled=True
    )
    sketch = lax.all_to_all(spread, "section", split_axis=1, concat_axis=0, tiled=True)
    term = lax.dot_general(vectors, omega, (NT, ((), ())), preferred_element_type=F32)
    tiles = jnp.moveaxis(term.reshape(4, nr, -1), 1, 0)
    piece = lax.all_to_all(tiles, "row", 0, 0, tiled=True).sum(0)
    probe = lax.all_to_all(jnp.broadcast_to(piece[None], (ns, *piece.shape)), "section", 0, 0, tiled=True)
    probe = jnp.moveaxis(probe, 0, 1).reshape(4, -1)
    probe = jnp.concatenate([probe, jnp.zeros_like(probe)], axis=0)
    gram, nxt = gram_call(sketch, ns, nr)
    inv = inverse(gram)
    width = vectors.shape[1] // ns
    mine = lax.dynamic_slice_in_dim(vectors, s * width, width, 1)
    return chain_call(sketch, nxt, inv, probe, basis, mine, ns, nr)


def solution(mesh):
    placed = (P("section", "row"), P("row", "section"), P(None, "row"))
    return jax.shard_map(
        body,
        mesh=mesh,
        in_specs=placed,
        out_specs=(P(None, ("row", "section")), P(None, "section")),
        check_vma=False,
    )
```

time: 978 us -> 410 us (0.42)
  other arithmetic: 357 us -> 56.3 us
  starting transfers between devices: 223 us -> 11.2 us
  Pallas kernels: 0 us -> 143 us
  local copies, waits for them, and re-layouts: 78.8 us -> 14 us
  waiting for transfers between devices: 197 us -> 140 us
  blocking collectives: 58.7 us -> 15.9 us
  matrix products: 45.1 us -> 13 us
    another operation x73 -> x6, other arithmetic: 350 us -> 34 us  [inverse(): factor = jnp.linalg.cholesky(gram)]
    pallas_call x0 -> x2, Pallas kernels: none -> 143 us  [the longest x1 116 us: chain_call(): pl.pallas_call(functools.partial(chain_kernel, ns, nr), out_shape=(jax.Sh...]
    all_to_all x19 -> x2, starting transfers between devices: 144 us -> 11.2 us  [the longest x1 6.49 us: body(): lax.all_to_all(spread, 'section', split_axis=1, concat_axis=0, tiled=True)]
    ppermute x15 -> x0, starting transfers between devices: 78.7 us -> none  [from_behind(): lax.ppermute(value, axis, [(source, source + steps) for source in range(i...]
    another operation x114 -> x9, local copies, waits for them, and re-layouts: 63.2 us -> 4.12 us  [the longest x112 63.2 us: factor_solve(): lax.linalg.triangular_solve(factor, half, left_side=True, lower=True, tra...]
    psum x2 -> x0, blocking collectives: 26.7 us -> none  [broadcast_by_axis(): x = lax.psum(x, axis)]
    reduce_scatter x1, waiting for transfers between devices: 68.9 us -> 45.3 us  [body(): lax.psum_scatter(jnp.dot(omega, every, preferred_element_type=F32), 'row'...]
    another operation x2 -> x3, other arithmetic: 0.99 us -> 19.9 us  [lower_solve(): lax.linalg.triangular_solve(factor, right, left_side=True, lower=True, tr...]
  transfers between devices with their start and end apart: 37 -> 4, of which waited for: 21 -> 3; matrix products, arithmetic and copies ran while one was open for 39% -> 2% of each run, Pallas kernels for 0% -> 0%
where the time goes in v1:
time: 410 us; the launch traced here: 409 us
  Pallas kernels  143 us (35%)
  waiting for transfers between devices  140 us (34%)
  other arithmetic  56.3 us (14%)
  blocking collectives  15.9 us (4%)
  between operations  15.5 us (4%)
  local copies, waits for them, and re-layouts  14 us (3%)
  matrix products  13 us (3%)
  starting transfers between devices  11.2 us (3%)
    pallas_call x1, Pallas kernels, chain_call(): pl.pallas_call(functools.partial(chain_kernel, ns, nr), out_shape=(jax.Sh...  116 us
    all_gather x1, waiting for transfers between devices, body(): every = lax.all_gather(basis, 'section', axis=1, tiled=True)  87.1 us
    reduce_scatter x1, waiting for transfers between devices, body(): lax.psum_scatter(jnp.dot(omega, every, preferred_element_type=F32), 'row'...  45.3 us
    another operation x6, other arithmetic, inverse(): factor = jnp.linalg.cholesky(gram)  34 us
    pallas_call x1, Pallas kernels, gram_call(): pl.pallas_call(functools.partial(gram_kernel, ns, nr), out_shape=(jax.Sha...  26.4 us
    another operation x3, other arithmetic, lower_solve(): lax.linalg.triangular_solve(factor, right, left_side=True, lower=True, tr...  19.9 us
    all_to_all x1, blocking collectives, body(): piece = lax.all_to_all(tiles, 'row', 0, 0, tiled=True).sum(0)  15.9 us
    dot_general x1, matrix products, body(): jnp.dot(omega, every, preferred_element_type=F32)  10 us
  transfers between devices with their start and end apart: 4, of which 3 were waited for; matrix products, arithmetic and copies ran while one was open for 2% of the time, Pallas kernels for 0%

profile of v1, /device:TPU:1, one launch (start us, length us, event | category | flops | bytes accessed | tf_op | source)
XLA Modules:
  0.0 408.8 jit_solution(4363957541124388268)
XLA Ops:
  7.2 0.0 copy-start
  7.2 0.0 all-gather.2.cloned.1.call-start
  7.2 0.7 all-gather.2.cloned.1.call-update
  7.9 0.0 reduce-scatter.2.cloned.1.call-start
  8.0 87.1 %all-gather.2.cloned.1.call-done = bf16[1024,4096]{1,0:T(8,128)(2,1)} async-done(((bf16[1024,256]{1,0:T(8,128)(2,1)}), bf16[1024,4096]{1,0:T(8,128)(2,1)}) %all-gather.2.cloned.1.call-update) | async-done | bytes 8388624 | tf_op jit(solution)/shard_map/all_gather | solution.py:365
  95.1 0.0 copy-done
  95.1 10.0 %fusion.14 = f32[512,4096]{1,0:T(8,128)} fusion(bf16[512,1024]{1,0:T(8,128)(2,1)S(1)} %copy-done, bf16[1024,4096]{1,0:T(8,128)(2,1)} %all-gather.2.cloned.1.call-done), kind=kOutput, calls=%fused_computation.37 | convolution fusion | flops 4294967296 | bytes 17825792 | tf_op jit(solution)/shard_map/dot_general | solution.py:367
  105.1 0.0 copy-start.2
  105.1 0.0 reduce-scatter.2.cloned.1.call-update
  105.1 0.7 copy-done.2
  105.8 0.4 fusion.15
  106.2 0.1 reshape.31
  106.3 0.1 reshape.52
  106.4 15.9 %all_to_all.29 = f32[16,1,128]{2,1,0:T(1,128)S(1)} all-to-all(f32[16,1,128]{2,1,0:T(1,128)S(1)} %reshape.52), channel_id=1, replica_groups=mesh['section'=16,'row'=16] {'row'}, dimensions={0} | all-to-all | bytes 16384 | tf_op jit(solution)/shard_map/all_to_all | solution.py:372
  122.3 0.6 broadcast.110
  122.9 0.6 reduce.12
  123.5 0.1 reshape.53
  123.6 0.7 reshape.54
  124.3 4.7 %all-to-all-start.2 = ((f32[16,1,128]{2,1,0:T(1,128)}), f32[16,1,128]{2,1,0:T(1,128)S(1)}, u32[]{:S(2)}, u32[]{:S(2)}) async-start(f32[16,1,128]{2,1,0:T(1,128)} %reshape.54), calls=%async_computation.3 | async-start | bytes 16384 | tf_op jit(solution)/shard_map/all_to_all | solution.py:373
  129.0 45.3 %reduce-scatter.2.cloned.1.call-done = f32[32,4096]{1,0:T(8,128)} async-done(((f32[512,4096]{1,0:T(8,128)}), f32[32,4096]{1,0:T(8,128)}) %reduce-scatter.2.cloned.1.call-update) | async-done | bytes 524304 | tf_op jit(solution)/shard_map/reduce_scatter | solution.py:366
  174.3 1.9 copy.14
  176.1 0.0 all-to-all-done.2
  176.1 6.5 %all-to-all-start = ((f32[32,16,256]{2,0,1:T(8,128)}), f32[32,16,256]{2,0,1:T(8,128)S(1)}, u32[]{:S(2)}, u32[]{:S(2)}) async-start(f32[32,16,256]{2,0,1:T(8,128)} %bitcast.38), calls=%async_computation.1 | async-start | bytes 1048576 | tf_op jit(solution)/shard_map/all_to_all | solution.py:369
  182.7 0.6 constant_dynamic-slice_fusion.1.vec_ref
  183.3 0.6 reduce.13
  184.0 0.1 reshape.55
  184.1 0.1 reshape.32
  184.2 0.6 concatenate.5.p0_ref
  184.8 7.1 %all-to-all-done = f32[32,16,256]{2,0,1:T(8,128)S(1)} async-done(((f32[32,16,256]{2,0,1:T(8,128)}), f32[32,16,256]{2,0,1:T(8,128)S(1)}, u32[]{:S(2)}, u32[]{:S(2)}) %all-to-all-start) | async-done | bytes 524320 | tf_op jit(solution)/shard_map/all_to_all | solution.py:369
  191.8 0.0 copy-start.1
  191.8 0.8 copy-done.1
  192.6 26.4 %shard_map.50 = (f32[256,256]{1,0:T(8,128)}, f32[512,256]{1,0:T(8,128)}) custom-call(f32[512,256]{1,0:T(8,128)} %bitcast.46), custom_call_target="tpu_custom_call" | custom-call | tf_op jit(solution)/shard_map/pallas_call | solution.py:102
  219.1 1.1 copy.8
  220.2 1.0 fusion.4
  221.2 11.7 %cholesky.50 = f32[128,128]{1,0:T(8,128)S(1)} custom-call(f32[128,128]{1,0:T(8,128)S(1)} %cholesky.118), custom_call_target="Cholesky" | custom-call | tf_op jit(solution)/shard_map/jit(cholesky)/cholesky | solution.py:357
  232.9 9.8 %custom-call.14 = f32[1,128,128]{1,2,0:T(8,128)S(1)} custom-call(f32[1,128,128]{2,1,0:T(8,128)S(1)} %get-tuple-element.27), custom_call_target="InvertDiagBlocksLowerTriangular" | custom-call | tf_op jit(solution)/shard_map/jit(cholesky)/cholesky | solution.py:357
  242.8 0.2 constant_dynamic-update-slice_fusion
  243.0 0.3 convolution_subtract_fusion.1
  243.2 11.7 %cholesky.105 = f32[128,128]{1,0:T(8,128)S(1)} custom-call(f32[128,128]{1,0:T(8,128)S(1)} %convolution_subtract_fusion.1), custom_call_target="Cholesky" | custom-call | tf_op jit(solution)/shard_map/jit(cholesky)/cholesky | solution.py:357
  255.0 0.7 compare_reduce_fusion
  257.0 0.1 triangular_solve.63
  257.1 4.1 while.1
  257.1 0.7 fusion.25
  257.7 1.3 bitcast_dynamic-update-slice_fusion.2
  259.1 0.7 fusion.25
  259.8 1.3 bitcast_dynamic-update-slice_fusion.2
  261.1 19.9 %custom-call.15 = f32[2,128,128]{1,2,0:T(8,128)S(1)} custom-call(f32[2,128,128]{2,1,0:T(8,128)S(1)} %get-tuple-element.13), custom_call_target="InvertDiagBlocksLowerTriangular" | custom-call | tf_op jit(solution)/shard_map/triangular_solve | solution.py:353
  281.0 0.3 fusion.5
  281.3 0.3 convolution_subtract_fusion
  281.6 0.3 fusion.8
  281.9 1.3 fusion.inv_ref
  283.2 116.3 %shard_map.51 = (f32[4,64]{1,0:T(4,128)}, f32[4,256]{1,0:T(4,128)}) custom-call(f32[512,256]{1,0:T(8,128)} %bitcast.47, f32[512,256]{1,0:T(8,128)} %get-tuple-element.4.next_ref, f32[256,256]{1,0:T(8,128)} %fusion.inv_ref, f32[8,512]{1,0:T(8,128)} %concatenate.5.p0_ref, bf16[1024,256]{1,0:T(8,128)(2,1)} %basis_ref.1, ...), custom_call_target="tpu_custom_call" | custom-call | tf_op jit(solution)/shard_map/pallas_call | solution.py:317
  399.5 1.3 copy.29
  400.7 1.3 copy.30
  (14 shorter events, 0.2 us)
Async XLA Ops:
  7.2 87.9 %copy-start = (bf16[512,1024]{1,0:T(8,128)(2,1)S(1)}, bf16[512,1024]{1,0:T(8,128)(2,1)}, u32[]{:S(2)}) copy-start(bf16[512,1024]{1,0:T(8,128)(2,1)} %param.3) | copy-start | bytes 3145732
  7.2 87.9 %all-gather.2.cloned.1.call-start = ((), (), s32[]{:S(2)}) async-start(), calls=%async_computation.4 | async-start | bytes 8912896 | tf_op jit(solution)/shard_map/all_gather | solution.py:365
  7.9 166.3 %reduce-scatter.2.cloned.1.call-start = ((), (), s32[]{:S(2)}) async-start(), calls=%async_computation.5 | async-start | bytes 8912896 | tf_op jit(solution)/shard_map/reduce_scatter | solution.py:366
  105.1 0.7 copy-start.2
  124.3 51.8 %all-to-all-start.2 = ((f32[16,1,128]{2,1,0:T(1,128)}), f32[16,1,128]{2,1,0:T(1,128)S(1)}, u32[]{:S(2)}, u32[]{:S(2)}) async-start(f32[16,1,128]{2,1,0:T(1,128)} %reshape.54), calls=%async_computation.3 | async-start | bytes 16384 | tf_op jit(solution)/shard_map/all_to_all | solution.py:373
  176.1 15.7 %all-to-all-start = ((f32[32,16,256]{2,0,1:T(8,128)}), f32[32,16,256]{2,0,1:T(8,128)S(1)}, u32[]{:S(2)}, u32[]{:S(2)}) async-start(f32[32,16,256]{2,0,1:T(8,128)} %bitcast.38), calls=%async_computation.1 | async-start | bytes 1048576 | tf_op jit(solution)/shard_map/all_to_all | solution.py:369
  191.8 0.8 copy-start.1
Sparse Core Ops, SparseCore 0:
  10.4 84.6 all-gather.1
  105.3 68.9 reduce-scatter.1

commit v2 on v1

--- a/solution.py
+++ b/solution.py
@@ -349,14 +349,58 @@
     )(sketch, nxt, inv, probe, basis, mine)
 
 
-def lower_solve(factor, right):
-    return lax.linalg.triangular_solve(factor, right, left_side=True, lower=True, transpose_a=False)
+def eliminate(a):
+    n = a.shape[0]
+    rows = lax.broadcasted_iota(jnp.int32, (n, n), 0)
+    cols = lax.broadcasted_iota(jnp.int32, (n, n), 1)
+    lane = lax.broadcasted_iota(jnp.int32, (1, n), 1)
+    for k in range(0, n, 2):
+        c1 = jnp.broadcast_to(a[:, k : k + 1], (n, n))
+        c2 = jnp.broadcast_to(a[:, k + 1 : k + 2], (n, n))
+        p, q, s = c1[k : k + 1], c2[k : k + 1], c2[k + 1 : k + 2]
+        e = 1.0 / (p * s - q * q)
+        r1 = jnp.where(lane == k, 1.0, jnp.where(lane == k + 1, 0.0, a[k : k + 1, :]))
+        r2 = jnp.where(lane == k + 1, 1.0, jnp.where(lane == k, 0.0, a[k + 1 : k + 2, :]))
+        w1 = (s * e) * r1 - (q * e) * r2
+        w2 = (p * e) * r2 - (q * e) * r1
+        base = jnp.where((cols == k) | (cols == k + 1), 0.0, a)
+        new = base - c1 * w1 - c2 * w2
+        last = jnp.where(rows == k + 1, jnp.broadcast_to(w2, (n, n)), new)
+        a = jnp.where(rows == k, jnp.broadcast_to(w1, (n, n)), last)
+    return a
+
+
+def inverse_kernel(g_ref, out_ref):
+    g = g_ref[...]
+    n = g.shape[0]
+    h = n // 2
+    eye = lax.broadcasted_iota(jnp.int32, (n, n), 0) == lax.broadcasted_iota(jnp.int32, (n, n), 1)
+    d = jnp.where(eye, g, 0.0)
+    rs = lax.rsqrt(jnp.sum(d, axis=1, keepdims=True))
+    cs = lax.rsqrt(jnp.sum(d, axis=0, keepdims=True))
+    g = g * rs * cs
+
+    def dot(x, y, dims):
+        return lax.dot_general(x, y, (dims, ((), ())), precision=HI, preferred_element_type=F32)
+
+    a, b, c = g[:h, :h], g[:h, h:], g[h:, h:]
+    ai = eliminate(a)
+    t = dot(ai, b, NN)
+    ci = eliminate(c - dot(b, t, TN))
+    u = dot(t, ci, NN)
+    top = jnp.concatenate([ai + dot(u, t, NT), -u], axis=1)
+    low = jnp.concatenate([-u.T, ci], axis=1)
+    out_ref[...] = jnp.concatenate([top, low], axis=0) * rs * cs
 
 
 def inverse(gram):
-    factor = jnp.linalg.cholesky(gram)
-    half = lower_solve(factor, jnp.eye(gram.shape[0], dtype=F32))
-    return jnp.dot(half.T, half, precision=HI)
+    vm = pl.BlockSpec(memory_space=pltpu.VMEM)
+    return pl.pallas_call(
+        inverse_kernel,
+        out_shape=jax.ShapeDtypeStruct(gram.shape, F32),
+        in_specs=[vm],
+        out_specs=vm,
+    )(gram)
 
 
 def body(omega, basis, vectors):

time: 410 us -> 362 us (0.88)
  other arithmetic: 56.3 us -> 1.36 us
  Pallas kernels: 143 us -> 159 us
  local copies, waits for them, and re-layouts: 14 us -> 8.79 us
    another operation x9 -> x0, other arithmetic: 54 us -> none  [the longest x6 34 us: inverse(): factor = jnp.linalg.cholesky(gram)]
    pallas_call x0 -> x1, Pallas kernels: none -> 16.9 us  [inverse(): pl.pallas_call(inverse_kernel, out_shape=jax.ShapeDtypeStruct(gram.shape,...]
    another operation x9 -> x0, local copies, waits for them, and re-layouts: 4.12 us -> none
where the time goes in v2:
time: 362 us
  Pallas kernels  159 us (44%)
  waiting for transfers between devices  140 us (39%)
  blocking collectives  15.9 us (4%)
  between operations  14.1 us (4%)
  starting transfers between devices  11.3 us (3%)
  matrix products  10.4 us (3%)
  local copies, waits for them, and re-layouts  8.79 us (2%)
    pallas_call x1, Pallas kernels, chain_call(): pl.pallas_call(functools.partial(chain_kernel, ns, nr), out_shape=(jax.Sh...  116 us
    all_gather x1, waiting for transfers between devices, body(): every = lax.all_gather(basis, 'section', axis=1, tiled=True)  87.1 us
    reduce_scatter x1, waiting for transfers between devices, body(): lax.psum_scatter(jnp.dot(omega, every, preferred_element_type=F32), 'row'...  45.3 us
    pallas_call x1, Pallas kernels, gram_call(): pl.pallas_call(functools.partial(gram_kernel, ns, nr), out_shape=(jax.Sha...  26.4 us
    pallas_call x1, Pallas kernels, inverse(): pl.pallas_call(inverse_kernel, out_shape=jax.ShapeDtypeStruct(gram.shape,...  16.9 us
    all_to_all x1, blocking collectives, body(): piece = lax.all_to_all(tiles, 'row', 0, 0, tiled=True).sum(0)  15.9 us
    dot_general x1, matrix products, body(): jnp.dot(omega, every, preferred_element_type=F32)  10 us
  transfers between devices with their start and end apart: 4, of which 3 were waited for; matrix products, arithmetic and copies ran while one was open for 2% of the time, Pallas kernels for 0%

profile of v2, /device:TPU:1, one launch (start us, length us, event | category | flops | bytes accessed | tf_op | source)
XLA Modules:
  0.0 361.5 jit_solution(11666572773409450570)
XLA Ops:
  7.2 0.0 copy-start
  7.2 0.0 all-gather.2.cloned.1.call-start
  7.2 0.7 all-gather.2.cloned.1.call-update
  7.9 0.0 reduce-scatter.2.cloned.1.call-start
  8.0 87.1 %all-gather.2.cloned.1.call-done = bf16[1024,4096]{1,0:T(8,128)(2,1)} async-done(((bf16[1024,256]{1,0:T(8,128)(2,1)}), bf16[1024,4096]{1,0:T(8,128)(2,1)}) %all-gather.2.cloned.1.call-update) | async-done | bytes 8388624 | tf_op jit(solution)/shard_map/all_gather | solution.py:409
  95.1 0.0 copy-done
  95.1 10.0 %fusion = f32[512,4096]{1,0:T(8,128)} fusion(bf16[512,1024]{1,0:T(8,128)(2,1)S(1)} %copy-done, bf16[1024,4096]{1,0:T(8,128)(2,1)} %all-gather.2.cloned.1.call-done), kind=kOutput, calls=%fused_computation.3 | convolution fusion | flops 4294967296 | bytes 17825792 | tf_op jit(solution)/shard_map/dot_general | solution.py:411
  105.1 0.0 copy-start.2
  105.1 0.0 reduce-scatter.2.cloned.1.call-update
  105.1 0.7 copy-done.2
  105.8 0.4 fusion.1
  106.2 0.1 reshape.14
  106.3 0.1 reshape.16
  106.4 15.9 %all_to_all.29 = f32[16,1,128]{2,1,0:T(1,128)S(1)} all-to-all(f32[16,1,128]{2,1,0:T(1,128)S(1)} %reshape.16), channel_id=1, replica_groups=mesh['section'=16,'row'=16] {'row'}, dimensions={0} | all-to-all | bytes 16384 | tf_op jit(solution)/shard_map/all_to_all | solution.py:416
  122.3 0.5 broadcast.3
  122.8 0.7 reduce
  123.5 0.1 reshape.17
  123.6 0.7 reshape.18
  124.3 4.7 %all-to-all-start.2 = ((f32[16,1,128]{2,1,0:T(1,128)}), f32[16,1,128]{2,1,0:T(1,128)S(1)}, u32[]{:S(2)}, u32[]{:S(2)}) async-start(f32[16,1,128]{2,1,0:T(1,128)} %reshape.18), calls=%async_computation.3 | async-start | bytes 16384 | tf_op jit(solution)/shard_map/all_to_all | solution.py:417
  129.0 45.3 %reduce-scatter.2.cloned.1.call-done = f32[32,4096]{1,0:T(8,128)} async-done(((f32[512,4096]{1,0:T(8,128)}), f32[32,4096]{1,0:T(8,128)}) %reduce-scatter.2.cloned.1.call-update) | async-done | bytes 524304 | tf_op jit(solution)/shard_map/reduce_scatter | solution.py:410
  174.3 1.9 copy.12
  176.1 0.0 all-to-all-done.2
  176.1 6.5 %all-to-all-start = ((f32[32,16,256]{2,0,1:T(8,128)}), f32[32,16,256]{2,0,1:T(8,128)S(1)}, u32[]{:S(2)}, u32[]{:S(2)}) async-start(f32[32,16,256]{2,0,1:T(8,128)} %bitcast.13), calls=%async_computation.1 | async-start | bytes 1048576 | tf_op jit(solution)/shard_map/all_to_all | solution.py:413
  182.7 0.6 constant_dynamic-slice_fusion.vec_ref
  183.3 0.7 reduce.1
  184.0 0.1 reshape.19
  184.1 0.1 reshape.15
  184.2 0.6 concatenate.3.p0_ref
  184.8 7.1 %all-to-all-done = f32[32,16,256]{2,0,1:T(8,128)S(1)} async-done(((f32[32,16,256]{2,0,1:T(8,128)}), f32[32,16,256]{2,0,1:T(8,128)S(1)}, u32[]{:S(2)}, u32[]{:S(2)}) %all-to-all-start) | async-done | bytes 524320 | tf_op jit(solution)/shard_map/all_to_all | solution.py:413
  191.9 0.0 copy-start.1
  191.9 0.8 copy-done.1
  192.7 26.4 %shard_map.50 = (f32[256,256]{1,0:T(8,128)}, f32[512,256]{1,0:T(8,128)}) custom-call(f32[512,256]{1,0:T(8,128)} %bitcast.15), custom_call_target="tpu_custom_call" | custom-call | tf_op jit(solution)/shard_map/pallas_call | solution.py:102
  219.1 16.9 %shard_map.51.inv_ref = f32[256,256]{1,0:T(8,128)} custom-call(f32[256,256]{1,0:T(8,128)} %get-tuple-element.5.g_ref), custom_call_target="tpu_custom_call" | custom-call | tf_op jit(solution)/shard_map/pallas_call | solution.py:398
  235.9 116.2 %shard_map.52 = (f32[4,64]{1,0:T(4,128)}, f32[4,256]{1,0:T(4,128)}) custom-call(f32[512,256]{1,0:T(8,128)} %bitcast.16, f32[512,256]{1,0:T(8,128)} %get-tuple-element.4.next_ref, f32[256,256]{1,0:T(8,128)} %shard_map.51.inv_ref, f32[8,512]{1,0:T(8,128)} %concatenate.3.p0_ref, bf16[1024,256]{1,0:T(8,128)(2,1)} %basis_ref.1, ...), custom_call_target="tpu_custom_call" | custom-call | tf_op jit(solution)/shard_map/pallas_call | solution.py:317
  352.2 1.2 copy.16
  353.4 1.3 copy.17
  (4 shorter events, 0.1 us)
Async XLA Ops:
  7.2 87.9 %copy-start = (bf16[512,1024]{1,0:T(8,128)(2,1)S(1)}, bf16[512,1024]{1,0:T(8,128)(2,1)}, u32[]{:S(2)}) copy-start(bf16[512,1024]{1,0:T(8,128)(2,1)} %param.3) | copy-start | bytes 3145732
  7.2 87.9 %all-gather.2.cloned.1.call-start = ((), (), s32[]{:S(2)}) async-start(), calls=%async_computation.4 | async-start | bytes 8912896 | tf_op jit(solution)/shard_map/all_gather | solution.py:409
  7.9 166.3 %reduce-scatter.2.cloned.1.call-start = ((), (), s32[]{:S(2)}) async-start(), calls=%async_computation.5 | async-start | bytes 8912896 | tf_op jit(solution)/shard_map/reduce_scatter | solution.py:410
  105.1 0.7 copy-start.2
  124.3 51.9 %all-to-all-start.2 = ((f32[16,1,128]{2,1,0:T(1,128)}), f32[16,1,128]{2,1,0:T(1,128)S(1)}, u32[]{:S(2)}, u32[]{:S(2)}) async-start(f32[16,1,128]{2,1,0:T(1,128)} %reshape.18), calls=%async_computation.3 | async-start | bytes 16384 | tf_op jit(solution)/shard_map/all_to_all | solution.py:417
  176.1 15.7 %all-to-all-start = ((f32[32,16,256]{2,0,1:T(8,128)}), f32[32,16,256]{2,0,1:T(8,128)S(1)}, u32[]{:S(2)}, u32[]{:S(2)}) async-start(f32[32,16,256]{2,0,1:T(8,128)} %bitcast.13), calls=%async_computation.1 | async-start | bytes 1048576 | tf_op jit(solution)/shard_map/all_to_all | solution.py:413
  191.9 0.8 copy-start.1
Sparse Core Ops, SparseCore 0:
  10.4 84.6 all-gather.1
  105.3 68.9 reduce-scatter.1

commit v3 on v2

--- a/solution.py
+++ b/solution.py
@@ -184,7 +184,7 @@
 
     @pl.when(s == 0)
     def _():
-        p = p0_ref[...]
+        p = p0_ref[...].T[:8]
         probe[...] = p
         cout[...] = packed(dot3(split(p), sp, NN))
         copies = []
@@ -403,25 +403,300 @@
     )(gram)
 
 
+def slot_offset(d):
+    return jnp.where(d == 0, 0, jnp.where(d == 1, 3, d - 1))
+
+
+def sketch_kernel(
+    nz,
+    omega_ref,
+    basis_ref,
+    vec_ref,
+    s_ref,
+    p_ref,
+    obuf,
+    bbuf,
+    keep,
+    give,
+    dbuf,
+    rbuf,
+    fbuf,
+    pbuf,
+    l_sem,
+    o_send,
+    o_recv,
+    b_send,
+    b_recv,
+    d_send,
+    d_recv,
+    r_send,
+    r_recv,
+    f_send,
+    f_recv,
+    p_send,
+    p_recv,
+):
+    s, r = lax.axis_index("section"), lax.axis_index("row")
+    y, x = lax.div(s, 4), lax.rem(s, 4)
+    z, c = lax.div(r, 2), lax.rem(r, 2)
+    units, hops = 17, nz - 1
+
+    def at(dy, dx):
+        return lax.rem(y + dy, 4) * 4 + lax.rem(x + dx, 4)
+
+    zp = lax.rem(z + 1, nz) * 2 + c
+    zm = lax.rem(z + nz - 1, nz) * 2 + c
+    mate = z * 2 + (1 - c)
+
+    local = [
+        pltpu.make_async_copy(basis_ref, bbuf.at[0], l_sem.at[0]),
+        pltpu.make_async_copy(omega_ref, obuf.at[0], l_sem.at[1]),
+        pltpu.make_async_copy(vec_ref, bbuf.at[4], l_sem.at[2]),
+    ]
+    for cp in local:
+        cp.start()
+
+    barrier = pltpu.get_barrier_semaphore()
+
+    def hello(section, row):
+        pl.semaphore_signal(barrier, inc=1, device_id=(section, row), device_id_type=MESH)
+
+    for dy, dx in ((1, 0), (3, 0), (0, 1), (0, 2), (0, 3)):
+        hello(at(dy, dx), r)
+    for row in (zp, zm, mate):
+        hello(s, row)
+
+    @pl.when(s == 0)
+    def _():
+        for t in range(1, 16):
+            hello(t, r)
+
+    for cp in local:
+        cp.wait()
+    pl.semaphore_wait(barrier, 8 + jnp.minimum(s, 1))
+
+    def ocopy(src, dst, half, sem, dy):
+        a, b = obuf.at[src], obuf.at[dst]
+        if half is not None:
+            a, b = a.at[pl.ds(4 * half, 4)], b.at[pl.ds(4 * half, 4)]
+        return remote(a, b, o_send.at[sem], o_recv.at[sem], at(dy, 0), r)
+
+    def bcopy(src, dst, half, sem, dx):
+        a, b = bbuf.at[src], bbuf.at[dst]
+        if half is not None:
+            a, b = a.at[pl.ds(512 * half, 512)], b.at[pl.ds(512 * half, 512)]
+        return remote(a, b, b_send.at[sem], b_recv.at[sem], at(0, dx), r)
+
+    b_own = [bcopy(0, 1, None, 0, 1), bcopy(0, 2, None, 1, 3)]
+    o_own = [ocopy(0, 1, None, 0, 1), ocopy(0, 2, None, 1, 3)]
+    b_fwd = [bcopy(1, 3, 0, 2, 1), bcopy(2, 3, 1, 3, 3)]
+    o_fwd = [ocopy(1, 3, 0, 2, 1), ocopy(2, 3, 1, 3, 3)]
+    for cp in b_own + o_own:
+        cp.start()
+
+    def dcopy(u):
+        return remote(give.at[u], dbuf.at[u], d_send.at[u], d_recv.at[u], s, mate)
+
+    def chunk(h, k):
+        return lax.rem(z + nz - 1 - k, nz) if h == 0 else lax.rem(z + 1 + k, nz)
+
+    def rcopy(u, h, k):
+        return remote(
+            keep.at[u, h, chunk(h, k)],
+            rbuf.at[u, h, k],
+            r_send.at[u, h, k],
+            r_recv.at[u, h, k],
+            s,
+            zp if h == 0 else zm,
+        )
+
+    def place(u):
+        v = u - 1
+        return slot_offset(lax.div(v, 4)), slot_offset(lax.rem(v, 4))
+
+    def fcopy(u):
+        dy, dx = place(u)
+        rows = pl.ds(pl.multiple_of((lax.rem(y + dy, 4) * 4 + x) * 32, 32), 32)
+        return remote(fbuf.at[u], s_ref.at[rows], f_send.at[u], f_recv.at[u], at(0, dx), r)
+
+    def pcopy(sender):
+        return remote(pbuf, p_ref.at[sender], p_send, p_recv.at[sender], 0, r)
+
+    def step(t, carry):
+        for k in range(hops, -1, -1):
+            u = t - 1 - k
+            for h in range(2):
+                first = 0 if h == 0 else 1
+
+                @pl.when((u >= first) & (u < units))
+                def _():
+                    if k == 0:
+                        if h == 0:
+                            dcopy(u).wait_recv()
+                    else:
+                        rcopy(u, h, k - 1).wait_recv()
+                    ch = chunk(h, k)
+                    val = keep[u, h, ch] + dbuf[u, h, ch]
+                    if k > 0:
+                        val = val + rbuf[u, h, k - 1]
+                    if k < hops:
+                        keep[u, h, ch] = val
+                        rcopy(u, h, k).start()
+                    else:
+                        fbuf[u, :, h * 128 : (h + 1) * 128] = val
+
+        done = t - 1 - hops
+
+        @pl.when((done >= 1) & (done < units))
+        def _():
+            dy, dx = place(done)
+
+            @pl.when(dx == 0)
+            def _():
+                rows = pl.ds(pl.multiple_of((lax.rem(y + dy, 4) * 4 + x) * 32, 32), 32)
+                s_ref[rows, :] = fbuf[done]
+
+            @pl.when(dx > 0)
+            def _():
+                fcopy(done).start()
+
+        @pl.when(done == 0)
+        def _():
+            @pl.when(s == 0)
+            def _():
+                p_ref[0] = fbuf[0, :, :128]
+
+            @pl.when(s > 0)
+            def _():
+                pbuf[...] = fbuf[0, :, :128]
+                pcopy(s).start()
+
+        @pl.when(t == 2)
+        def _():
+            for cp in b_own:
+                cp.wait_recv()
+            for cp in b_fwd:
+                cp.start()
+
+        @pl.when(t == 4)
+        def _():
+            for cp in b_fwd:
+                cp.wait_recv()
+
+        @pl.when(t == 5)
+        def _():
+            for cp in o_own:
+                cp.wait_recv()
+            for cp in o_fwd:
+                cp.start()
+
+        @pl.when(t == 13)
+        def _():
+            for cp in o_fwd:
+                cp.wait_recv()
+
+        @pl.when(t < units)
+        def _():
+            v = jnp.maximum(t - 1, 0)
+            oslot = lax.div(v, 4)
+            bslot = jnp.where(t == 0, 4, lax.rem(v, 4))
+            b = bbuf[bslot]
+            for which, dst in ((1 - c, give), (c, keep)):
+                o = obuf[oslot, :, which].reshape(256, 1024)
+                out = jnp.dot(o, b, preferred_element_type=F32)
+                for h in range(2):
+                    dst[t, h] = out[:, h * 128 : (h + 1) * 128].reshape(8, 32, 128)
+                if dst is give:
+                    dcopy(t).start()
+
+        return carry
+
+    lax.fori_loop(0, units + nz, step, 0)
+
+    for u in range(1, units):
+        if (u - 1) % 4:
+            fcopy(u).wait()
+
+    @pl.when(s == 0)
+    def _():
+        for t in range(1, 16):
+            pcopy(t).wait_recv()
+
+    @pl.when(s > 0)
+    def _():
+        pcopy(s).wait_send()
+
+    for cp in b_own + o_own + b_fwd + o_fwd:
+        cp.wait_send()
+
+    def drain(u, carry):
+        dcopy(u).wait_send()
+        for h in range(2):
+            for k in range(hops):
+
+                @pl.when(u >= h)
+                def _():
+                    rcopy(u, h, k).wait_send()
+
+        return carry
+
+    lax.fori_loop(0, units, drain, 0)
+
+
+def sketch_call(omega, basis, vecs, nr):
+    vm = pl.BlockSpec(memory_space=pltpu.VMEM)
+    anym = pl.BlockSpec(memory_space=pl.ANY)
+    dma = pltpu.SemaphoreType.DMA
+    nz = nr // 2
+    m, k = omega.shape
+    n = basis.shape[1]
+    part = m // nr
+    units = 17
+    return pl.pallas_call(
+        functools.partial(sketch_kernel, nz),
+        out_shape=(
+            jax.ShapeDtypeStruct((m, n), F32),
+            jax.ShapeDtypeStruct((16, part, 128), F32),
+        ),
+        in_specs=[anym] * 3,
+        out_specs=(vm, vm),
+        scratch_shapes=[
+            pltpu.VMEM((4, nz, 2, part, k), BF16),
+            pltpu.VMEM((5, k, n), BF16),
+            pltpu.VMEM((units, 2, nz, part, 128), F32),
+            pltpu.VMEM((units, 2, nz, part, 128), F32),
+            pltpu.VMEM((units, 2, nz, part, 128), F32),
+            pltpu.VMEM((units, 2, nz - 1, part, 128), F32),
+            pltpu.VMEM((units, part, n), F32),
+            pltpu.VMEM((part, 128), F32),
+            dma((3,)),
+            dma((4,)),
+            dma((4,)),
+            dma((4,)),
+            dma((4,)),
+            dma((units,)),
+            dma((units,)),
+            dma((units, 2, nz - 1)),
+            dma((units, 2, nz - 1)),
+            dma((units,)),
+            dma((units,)),
+            dma,
+            dma((16,)),
+        ],
+        compiler_params=pltpu.CompilerParams(collective_id=2, has_side_effects=True),
+    )(omega.reshape(nz, 2, part, k), basis, vecs)
+
+
 def body(omega, basis, vectors):
     ns, nr = lax.axis_size("section"), lax.axis_size("row")
     s = lax.axis_index("section")
-    every = lax.all_gather(basis, "section", axis=1, tiled=True)
-    spread = lax.psum_scatter(
-        jnp.dot(omega, every, preferred_element_type=F32), "row", scatter_dimension=0, tiled=True
-    )
-    sketch = lax.all_to_all(spread, "section", split_axis=1, concat_axis=0, tiled=True)
-    term = lax.dot_general(vectors, omega, (NT, ((), ())), preferred_element_type=F32)
-    tiles = jnp.moveaxis(term.reshape(4, nr, -1), 1, 0)
-    piece = lax.all_to_all(tiles, "row", 0, 0, tiled=True).sum(0)
-    probe = lax.all_to_all(jnp.broadcast_to(piece[None], (ns, *piece.shape)), "section", 0, 0, tiled=True)
-    probe = jnp.moveaxis(probe, 0, 1).reshape(4, -1)
-    probe = jnp.concatenate([probe, jnp.zeros_like(probe)], axis=0)
+    vecs = jnp.pad(vectors.T, ((0, 0), (0, basis.shape[1] - vectors.shape[0])))
+    sketch, probe = sketch_call(omega, basis, vecs, nr)
     gram, nxt = gram_call(sketch, ns, nr)
     inv = inverse(gram)
     width = vectors.shape[1] // ns
     mine = lax.dynamic_slice_in_dim(vectors, s * width, width, 1)
-    return chain_call(sketch, nxt, inv, probe, basis, mine, ns, nr)
+    return chain_call(sketch, nxt, inv, probe.reshape(-1, 128), basis, mine, ns, nr)
 
 
 def solution(mesh):

time: 362 us -> 271 us (0.75)
  waiting for transfers between devices: 140 us -> 0 us
  Pallas kernels: 159 us -> 265 us
  blocking collectives: 15.9 us -> 0 us
  between operations: 14.1 us -> 0.67 us
  starting transfers between devices: 11.3 us -> 0 us
  matrix products: 10.4 us -> 0 us
  local copies, waits for them, and re-layouts: 8.79 us -> 4.93 us
    pallas_call x0 -> x1, Pallas kernels: none -> 101 us  [sketch_call(): pl.pallas_call(functools.partial(sketch_kernel, nz), out_shape=(jax.Shape...]
    all_gather x1 -> x0, waiting for transfers between devices: 87.1 us -> none  [body(): every = lax.all_gather(basis, 'section', axis=1, tiled=True)]
    reduce_scatter x1 -> x0, waiting for transfers between devices: 45.3 us -> none  [body(): lax.psum_scatter(jnp.dot(omega, every, preferred_element_type=F32), 'row'...]
    all_to_all x1 -> x0, blocking collectives: 15.9 us -> none  [body(): piece = lax.all_to_all(tiles, 'row', 0, 0, tiled=True).sum(0)]
    all_to_all x2 -> x0, starting transfers between devices: 11.2 us -> none  [the longest x1 6.52 us: body(): lax.all_to_all(spread, 'section', split_axis=1, concat_axis=0, tiled=True)]
    dot_general x2 -> x0, matrix products: 10.4 us -> none  [the longest x1 10 us: body(): jnp.dot(omega, every, preferred_element_type=F32)]
    all_to_all x2 -> x0, waiting for transfers between devices: 7.12 us -> none  [the longest x1 7.11 us: body(): lax.all_to_all(spread, 'section', split_axis=1, concat_axis=0, tiled=True)]
  transfers between devices with their start and end apart: 4 -> 0, of which waited for: 3 -> 0; matrix products, arithmetic and copies ran while one was open for 2% -> 0% of each run, Pallas kernels for 0% -> 0%
where the time goes in v3:
time: 271 us
  Pallas kernels  265 us (98%)
  local copies, waits for them, and re-layouts  4.93 us (2%)
    pallas_call x1, Pallas kernels, chain_call(): pl.pallas_call(functools.partial(chain_kernel, ns, nr), out_shape=(jax.Sh...  117 us
    pallas_call x1, Pallas kernels, sketch_call(): pl.pallas_call(functools.partial(sketch_kernel, nz), out_shape=(jax.Shape...  101 us
    pallas_call x1, Pallas kernels, gram_call(): pl.pallas_call(functools.partial(gram_kernel, ns, nr), out_shape=(jax.Sha...  29.9 us
    pallas_call x1, Pallas kernels, inverse(): pl.pallas_call(inverse_kernel, out_shape=jax.ShapeDtypeStruct(gram.shape,...  16.9 us

profile of v3, /device:TPU:1, one launch (start us, length us, event | category | flops | bytes accessed | tf_op | source)
XLA Modules:
  0.0 270.6 jit_solution(2845861129889360611)
XLA Ops:
  0.6 0.9 copy.5
  1.5 0.9 pad.4.vec_ref
  2.4 101.3 %shard_map.50 = (f32[512,256]{1,0:T(8,128)}, f32[16,32,128]{2,1,0:T(8,128)}) custom-call(bf16[8,2,32,1024]{3,2,1,0:T(8,128)(2,1)} %bitcast.3, bf16[1024,256]{1,0:T(8,128)(2,1)} %basis_ref.3, bf16[1024,256]{1,0:T(8,128)(2,1)} %pad.4.vec_ref), custom_call_target="tpu_custom_call" | custom-call | tf_op jit(solution)/shard_map/pallas_call | solution.py:655
  103.7 29.9 %shard_map.51 = (f32[256,256]{1,0:T(8,128)}, f32[512,256]{1,0:T(8,128)}) custom-call(f32[512,256]{1,0:T(8,128)} %get-tuple-element.6.s_ref), custom_call_target="tpu_custom_call" | custom-call | tf_op jit(solution)/shard_map/pallas_call | solution.py:102
  133.6 16.9 %shard_map.52.inv_ref = f32[256,256]{1,0:T(8,128)} custom-call(f32[256,256]{1,0:T(8,128)} %get-tuple-element.8.g_ref), custom_call_target="tpu_custom_call" | custom-call | tf_op jit(solution)/shard_map/pallas_call | solution.py:398
  150.5 1.3 constant_dynamic-slice_fusion.vec_ref
  151.8 117.0 %shard_map.53 = (f32[4,64]{1,0:T(4,128)}, f32[4,256]{1,0:T(4,128)}) custom-call(f32[512,256]{1,0:T(8,128)} %get-tuple-element.6.s_ref, f32[512,256]{1,0:T(8,128)} %get-tuple-element.7.next_ref, f32[256,256]{1,0:T(8,128)} %shard_map.52.inv_ref, f32[512,128]{1,0:T(8,128)} %bitcast.5, bf16[1024,256]{1,0:T(8,128)(2,1)} %basis_ref.3, ...), custom_call_target="tpu_custom_call" | custom-call | tf_op jit(solution)/shard_map/pallas_call | solution.py:317
  268.7 0.0 copy-start
  268.8 1.3 copy.8
  270.0 0.0 copy-done
  270.0 0.6 copy.9
Async XLA Ops:
  268.7 1.3 copy-start

commit v4 on v3

--- a/solution.py
+++ b/solution.py
@@ -143,7 +143,8 @@
     vec_ref,
     ortho_ref,
     coef_ref,
-    cross,
+    hi_ref,
+    lo_ref,
     probe,
     moved,
     cout,
@@ -179,12 +180,12 @@
     sp = split(s_ref[...])
     nx = split(next_ref[...])
     iv = split(inv_ref[...])
-    cross[...] = dot3(sp, nx, TN)
+    hi_ref[...], lo_ref[...] = split(dot3(iv, split(dot3(sp, nx, TN)), NN))
     pl.semaphore_wait(barrier, 3 * nr + ns - 2)
 
     @pl.when(s == 0)
     def _():
-        p = p0_ref[...].T[:8]
+        p = p0_ref[:, :128].T[:8]
         probe[...] = p
         cout[...] = packed(dot3(split(p), sp, NN))
         copies = []
@@ -216,15 +217,16 @@
     for q in range(1, nr):
         total = total + cin[q]
     inner = unpacked(total)
-    coef = dot3(split(inner), iv, NN)
-    cs = split(coef)
+    cin_parts = split(inner)
 
     @pl.when(s < ns - 1)
     def _():
-        cout[...] = packed(ahead - dot3(cs, split(cross[...]), NN))
+        cout[...] = packed(ahead - dot3(cin_parts, (hi_ref[...], lo_ref[...]), NN))
         for q in range(nr):
             remote(cout, cin.at[r], c_send.at[q], c_recv.at[r], after, q).start()
 
+    coef = dot3(cin_parts, iv, NN)
+    cs = split(coef)
     moved[...] = p - dot3(cs, sp, NT)
 
     @pl.when(s < ns - 1)
@@ -323,7 +325,8 @@
         in_specs=[vm] * 6,
         out_specs=(vm, vm),
         scratch_shapes=[
-            pltpu.VMEM((n, n), F32),
+            pltpu.VMEM((n, n), BF16),
+            pltpu.VMEM((n, n), BF16),
             pltpu.VMEM((8, k), F32),
             pltpu.VMEM((8, k), F32),
             pltpu.VMEM((8, 128), F32),
@@ -403,8 +406,35 @@
     )(gram)
 
 
+def within(t, first, yes, no):
+    return jnp.where(t >= first, yes, no)
+
+
+def unit(t):
+    def seg(first, width):
+        return lax.div(jnp.maximum(t - first, 0), width), lax.rem(jnp.maximum(t - first, 0), width)
+
+    a, b = seg(4, 2)
+    row, half, col = within(t, 2, 0, 0), lax.rem(t, 2), within(t, 2, 0, 4)
+    row, half, col = row, within(t, 4, b, half), within(t, 4, 1 + a, col)
+    a, b = seg(8, 3)
+    row, half, col = within(t, 8, 1 + a, row), within(t, 8, a, half), within(t, 8, b, col)
+    row, half, col = within(t, 14, 0, row), within(t, 14, t - 14, half), within(t, 14, 3, col)
+    row, half, col = within(t, 16, t - 15, row), within(t, 16, t - 16, half), within(t, 16, 3, col)
+    a, b = seg(18, 4)
+    row, half, col = within(t, 18, 1 + a, row), within(t, 18, 1 - a, half), within(t, 18, b, col)
+    a, b = seg(26, 4)
+    row, half, col = within(t, 26, 3, row), within(t, 26, a, half), within(t, 26, b, col)
+    return row, half, col
+
+
 def slot_offset(d):
     return jnp.where(d == 0, 0, jnp.where(d == 1, 3, d - 1))
+
+
+UNITS = 34
+REACH = 4
+LAG = 3
 
 
 def sketch_kernel(
@@ -416,12 +446,10 @@
     p_ref,
     obuf,
     bbuf,
-    keep,
-    give,
+    part,
     dbuf,
     rbuf,
     fbuf,
-    pbuf,
     l_sem,
     o_send,
     o_recv,
@@ -439,18 +467,16 @@
     s, r = lax.axis_index("section"), lax.axis_index("row")
     y, x = lax.div(s, 4), lax.rem(s, 4)
     z, c = lax.div(r, 2), lax.rem(r, 2)
-    units, hops = 17, nz - 1
 
     def at(dy, dx):
         return lax.rem(y + dy, 4) * 4 + lax.rem(x + dx, 4)
 
-    zp = lax.rem(z + 1, nz) * 2 + c
-    zm = lax.rem(z + nz - 1, nz) * 2 + c
+    beside = (lax.rem(z + 1, nz) * 2 + c, lax.rem(z + nz - 1, nz) * 2 + c)
     mate = z * 2 + (1 - c)
 
     local = [
-        pltpu.make_async_copy(basis_ref, bbuf.at[0], l_sem.at[0]),
-        pltpu.make_async_copy(omega_ref, obuf.at[0], l_sem.at[1]),
+        pltpu.make_async_copy(omega_ref, obuf.at[0], l_sem.at[0]),
+        pltpu.make_async_copy(basis_ref, bbuf.at[0], l_sem.at[1]),
         pltpu.make_async_copy(vec_ref, bbuf.at[4], l_sem.at[2]),
     ]
     for cp in local:
@@ -463,7 +489,7 @@
 
     for dy, dx in ((1, 0), (3, 0), (0, 1), (0, 2), (0, 3)):
         hello(at(dy, dx), r)
-    for row in (zp, zm, mate):
+    for row in (*beside, mate):
         hello(s, row)
 
     @pl.when(s == 0)
@@ -476,10 +502,7 @@
     pl.semaphore_wait(barrier, 8 + jnp.minimum(s, 1))
 
     def ocopy(src, dst, half, sem, dy):
-        a, b = obuf.at[src], obuf.at[dst]
-        if half is not None:
-            a, b = a.at[pl.ds(4 * half, 4)], b.at[pl.ds(4 * half, 4)]
-        return remote(a, b, o_send.at[sem], o_recv.at[sem], at(dy, 0), r)
+        return remote(obuf.at[src, half], obuf.at[dst, half], o_send.at[sem], o_recv.at[sem], at(dy, 0), r)
 
     def bcopy(src, dst, half, sem, dx):
         a, b = bbuf.at[src], bbuf.at[dst]
@@ -488,159 +511,201 @@
         return remote(a, b, b_send.at[sem], b_recv.at[sem], at(0, dx), r)
 
     b_own = [bcopy(0, 1, None, 0, 1), bcopy(0, 2, None, 1, 3)]
-    o_own = [ocopy(0, 1, None, 0, 1), ocopy(0, 2, None, 1, 3)]
+    o_own = [ocopy(0, 1, 0, 0, 1), ocopy(0, 2, 1, 1, 3)]
+    o_rest = [ocopy(0, 1, 1, 2, 1), ocopy(0, 2, 0, 3, 3)]
     b_fwd = [bcopy(1, 3, 0, 2, 1), bcopy(2, 3, 1, 3, 3)]
-    o_fwd = [ocopy(1, 3, 0, 2, 1), ocopy(2, 3, 1, 3, 3)]
-    for cp in b_own + o_own:
+    o_fwd = [ocopy(1, 3, 0, 4, 1), ocopy(2, 3, 1, 5, 3)]
+    for cp in o_own + b_own + o_rest:
         cp.start()
 
     def dcopy(u):
-        return remote(give.at[u], dbuf.at[u], d_send.at[u], d_recv.at[u], s, mate)
-
-    def chunk(h, k):
-        return lax.rem(z + nz - 1 - k, nz) if h == 0 else lax.rem(z + 1 + k, nz)
-
-    def rcopy(u, h, k):
+        return remote(part.at[u, :, 1 - c], dbuf.at[u], d_send.at[u], d_recv.at[u], s, mate)
+
+    def chunk(d, k):
+        far = REACH - k
+        return lax.rem(z + (far if d == 0 else nz - far), nz)
+
+    def rcopy(u, d, k):
         return remote(
-            keep.at[u, h, chunk(h, k)],
-            rbuf.at[u, h, k],
-            r_send.at[u, h, k],
-            r_recv.at[u, h, k],
+            part.at[u, chunk(d, k), c],
+            rbuf.at[u, d, k],
+            r_send.at[u, d, k],
+            r_recv.at[u, d, k],
             s,
-            zp if h == 0 else zm,
+            beside[d],
         )
 
     def place(u):
-        v = u - 1
-        return slot_offset(lax.div(v, 4)), slot_offset(lax.rem(v, 4))
+        row, half, col = unit(u)
+        dy, dx = slot_offset(row), slot_offset(col)
+        start = (lax.rem(y + dy, 4) * 4 + x) * 32 + half * 16
+        return dx, pl.ds(pl.multiple_of(start, 16), 16)
 
     def fcopy(u):
-        dy, dx = place(u)
-        rows = pl.ds(pl.multiple_of((lax.rem(y + dy, 4) * 4 + x) * 32, 32), 32)
+        dx, rows = place(u)
         return remote(fbuf.at[u], s_ref.at[rows], f_send.at[u], f_recv.at[u], at(0, dx), r)
 
-    def pcopy(sender):
-        return remote(pbuf, p_ref.at[sender], p_send, p_recv.at[sender], 0, r)
+    def pcopy(u, sender):
+        return remote(fbuf.at[u], p_ref.at[sender, u], p_send.at[u], p_recv.at[sender, u], 0, r)
 
     def step(t, carry):
-        for k in range(hops, -1, -1):
-            u = t - 1 - k
-            for h in range(2):
-                first = 0 if h == 0 else 1
-
-                @pl.when((u >= first) & (u < units))
-                def _():
-                    if k == 0:
-                        if h == 0:
-                            dcopy(u).wait_recv()
-                    else:
-                        rcopy(u, h, k - 1).wait_recv()
-                    ch = chunk(h, k)
-                    val = keep[u, h, ch] + dbuf[u, h, ch]
-                    if k > 0:
-                        val = val + rbuf[u, h, k - 1]
-                    if k < hops:
-                        keep[u, h, ch] = val
-                        rcopy(u, h, k).start()
-                    else:
-                        fbuf[u, :, h * 128 : (h + 1) * 128] = val
-
-        done = t - 1 - hops
-
-        @pl.when((done >= 1) & (done < units))
-        def _():
-            dy, dx = place(done)
+        done = t - 2 - LAG * REACH
+
+        @pl.when((done >= 0) & (done < UNITS))
+        def _():
+            rcopy(done, 0, REACH - 1).wait_recv()
+            rcopy(done, 1, REACH - 1).wait_recv()
+            fbuf[done] = (part[done, z, c] + dbuf[done, z]) + (
+                rbuf[done, 0, REACH - 1] + rbuf[done, 1, REACH - 1]
+            )
+
+        @pl.when((done >= 2) & (done < UNITS))
+        def _():
+            dx, rows = place(done)
 
             @pl.when(dx == 0)
             def _():
-                rows = pl.ds(pl.multiple_of((lax.rem(y + dy, 4) * 4 + x) * 32, 32), 32)
                 s_ref[rows, :] = fbuf[done]
 
             @pl.when(dx > 0)
             def _():
                 fcopy(done).start()
 
-        @pl.when(done == 0)
+        @pl.when((done >= 0) & (done < 2))
         def _():
             @pl.when(s == 0)
             def _():
-                p_ref[0] = fbuf[0, :, :128]
+                p_ref[0, done] = fbuf[done]
 
             @pl.when(s > 0)
             def _():
-                pbuf[...] = fbuf[0, :, :128]
-                pcopy(s).start()
-
-        @pl.when(t == 2)
+                pcopy(done, s).start()
+
+        for k in range(REACH - 1, -1, -1):
+            u = t - 2 - LAG * k
+            valid = (u >= 0) & (u < UNITS)
+            if k == 0:
+
+                @pl.when(valid)
+                def _():
+                    dcopy(u).wait_recv()
+
+            for d in range(2):
+                longer = lax.rem(jnp.maximum(u, 0), 2) == d
+
+                def own():
+                    return part[u, chunk(d, k), c] + dbuf[u, chunk(d, k)]
+
+                def send(val):
+                    part[u, chunk(d, k), c] = val
+                    rcopy(u, d, k).start()
+
+                def pass_on():
+                    rcopy(u, d, k - 1).wait_recv()
+                    send(own() + rbuf[u, d, k - 1])
+
+                if k == 0:
+
+                    @pl.when(valid & longer)
+                    def _():
+                        send(own())
+
+                elif k == 1:
+
+                    @pl.when(valid & longer)
+                    def _():
+                        pass_on()
+
+                    @pl.when(valid & jnp.logical_not(longer))
+                    def _():
+                        send(own())
+
+                else:
+
+                    @pl.when(valid)
+                    def _():
+                        pass_on()
+
+        @pl.when(t == 4)
         def _():
             for cp in b_own:
                 cp.wait_recv()
             for cp in b_fwd:
                 cp.start()
 
-        @pl.when(t == 4)
-        def _():
-            for cp in b_fwd:
-                cp.wait_recv()
-
-        @pl.when(t == 5)
+        @pl.when(t == 8)
         def _():
             for cp in o_own:
                 cp.wait_recv()
             for cp in o_fwd:
                 cp.start()
 
-        @pl.when(t == 13)
+        @pl.when(t == 14)
+        def _():
+            for cp in b_fwd:
+                cp.wait_recv()
+
+        @pl.when(t == 18)
+        def _():
+            for cp in o_rest:
+                cp.wait_recv()
+
+        @pl.when(t == 26)
         def _():
             for cp in o_fwd:
                 cp.wait_recv()
 
-        @pl.when(t < units)
-        def _():
-            v = jnp.maximum(t - 1, 0)
-            oslot = lax.div(v, 4)
-            bslot = jnp.where(t == 0, 4, lax.rem(v, 4))
-            b = bbuf[bslot]
-            for which, dst in ((1 - c, give), (c, keep)):
-                o = obuf[oslot, :, which].reshape(256, 1024)
-                out = jnp.dot(o, b, preferred_element_type=F32)
-                for h in range(2):
-                    dst[t, h] = out[:, h * 128 : (h + 1) * 128].reshape(8, 32, 128)
-                if dst is give:
-                    dcopy(t).start()
+        @pl.when(t < UNITS)
+        def _():
+            row, half, col = unit(t)
+            out = jnp.dot(obuf[row, half], bbuf[col], preferred_element_type=F32)
+            part[t] = out.reshape(part.shape[1:])
+            dcopy(t).start()
 
         return carry
 
-    lax.fori_loop(0, units + nz, step, 0)
-
-    for u in range(1, units):
-        if (u - 1) % 4:
+    lax.fori_loop(0, UNITS + 2 + LAG * REACH + 1, step, 0)
+
+    def finish(u, carry):
+        dx, _ = place(u)
+
+        @pl.when(dx > 0)
+        def _():
             fcopy(u).wait()
 
+        return carry
+
+    lax.fori_loop(2, UNITS, finish, 0)
+
     @pl.when(s == 0)
     def _():
         for t in range(1, 16):
-            pcopy(t).wait_recv()
+            for u in range(2):
+                pcopy(u, t).wait_recv()
 
     @pl.when(s > 0)
     def _():
-        pcopy(s).wait_send()
-
-    for cp in b_own + o_own + b_fwd + o_fwd:
+        for u in range(2):
+            pcopy(u, s).wait_send()
+
+    for cp in b_own + o_own + o_rest + b_fwd + o_fwd:
         cp.wait_send()
 
     def drain(u, carry):
         dcopy(u).wait_send()
-        for h in range(2):
-            for k in range(hops):
-
-                @pl.when(u >= h)
-                def _():
-                    rcopy(u, h, k).wait_send()
+        for d in range(2):
+            for k in range(REACH):
+                if k:
+                    rcopy(u, d, k).wait_send()
+                else:
+
+                    @pl.when(lax.rem(u, 2) == d)
+                    def _():
+                        rcopy(u, d, k).wait_send()
 
         return carry
 
-    lax.fori_loop(0, units, drain, 0)
+    lax.fori_loop(0, UNITS, drain, 0)
 
 
 def sketch_call(omega, basis, vecs, nr):
@@ -650,41 +715,38 @@
     nz = nr // 2
     m, k = omega.shape
     n = basis.shape[1]
-    part = m // nr
-    units = 17
+    piece = m // nr // 2
     return pl.pallas_call(
         functools.partial(sketch_kernel, nz),
         out_shape=(
             jax.ShapeDtypeStruct((m, n), F32),
-            jax.ShapeDtypeStruct((16, part, 128), F32),
+            jax.ShapeDtypeStruct((16, 2, piece, n), F32),
         ),
         in_specs=[anym] * 3,
         out_specs=(vm, vm),
         scratch_shapes=[
-            pltpu.VMEM((4, nz, 2, part, k), BF16),
+            pltpu.VMEM((4, 2, m // 2, k), BF16),
             pltpu.VMEM((5, k, n), BF16),
-            pltpu.VMEM((units, 2, nz, part, 128), F32),
-            pltpu.VMEM((units, 2, nz, part, 128), F32),
-            pltpu.VMEM((units, 2, nz, part, 128), F32),
-            pltpu.VMEM((units, 2, nz - 1, part, 128), F32),
-            pltpu.VMEM((units, part, n), F32),
-            pltpu.VMEM((part, 128), F32),
+            pltpu.VMEM((UNITS, nz, 2, piece, n), F32),
+            pltpu.VMEM((UNITS, nz, piece, n), F32),
+            pltpu.VMEM((UNITS, 2, REACH, piece, n), F32),
+            pltpu.VMEM((UNITS, piece, n), F32),
             dma((3,)),
+            dma((6,)),
+            dma((6,)),
             dma((4,)),
             dma((4,)),
-            dma((4,)),
-            dma((4,)),
-            dma((units,)),
-            dma((units,)),
-            dma((units, 2, nz - 1)),
-            dma((units, 2, nz - 1)),
-            dma((units,)),
-            dma((units,)),
-            dma,
-            dma((16,)),
+            dma((UNITS,)),
+            dma((UNITS,)),
+            dma((UNITS, 2, REACH)),
+            dma((UNITS, 2, REACH)),
+            dma((UNITS,)),
+            dma((UNITS,)),
+            dma((2,)),
+            dma((16, 2)),
         ],
         compiler_params=pltpu.CompilerParams(collective_id=2, has_side_effects=True),
-    )(omega.reshape(nz, 2, part, k), basis, vecs)
+    )(omega.reshape(2, m // 2, k), basis, vecs)
 
 
 def body(omega, basis, vectors):
@@ -696,7 +758,7 @@
     inv = inverse(gram)
     width = vectors.shape[1] // ns
     mine = lax.dynamic_slice_in_dim(vectors, s * width, width, 1)
-    return chain_call(sketch, nxt, inv, probe.reshape(-1, 128), basis, mine, ns, nr)
+    return chain_call(sketch, nxt, inv, probe.reshape(-1, probe.shape[-1]), basis, mine, ns, nr)
 
 
 def solution(mesh):

time: 271 us -> 244 us (0.900)
  Pallas kernels: 265 us -> 238 us
    pallas_call x1, Pallas kernels: 101 us -> 80.6 us  [sketch_call(): pl.pallas_call(functools.partial(sketch_kernel, nz), out_shape=(jax.Shape...]
    pallas_call x1, Pallas kernels: 29.9 us -> 26.1 us  [gram_call(): pl.pallas_call(functools.partial(gram_kernel, ns, nr), out_shape=(jax.Sha...]
where the time goes in v4:
time: 244 us
  Pallas kernels  238 us (98%)
  local copies, waits for them, and re-layouts  4.95 us (2%)
    pallas_call x1, Pallas kernels, chain_call(): pl.pallas_call(functools.partial(chain_kernel, ns, nr), out_shape=(jax.Sh...  115 us
    pallas_call x1, Pallas kernels, sketch_call(): pl.pallas_call(functools.partial(sketch_kernel, nz), out_shape=(jax.Shape...  80.6 us
    pallas_call x1, Pallas kernels, gram_call(): pl.pallas_call(functools.partial(gram_kernel, ns, nr), out_shape=(jax.Sha...  26.1 us
    pallas_call x1, Pallas kernels, inverse(): pl.pallas_call(inverse_kernel, out_shape=jax.ShapeDtypeStruct(gram.shape,...  16.9 us

profile of v4, /device:TPU:1, one launch (start us, length us, event | category | flops | bytes accessed | tf_op | source)
XLA Modules:
  0.0 243.9 jit_solution(2304441991039917196)
XLA Ops:
  0.6 0.9 copy.5
  1.5 0.9 pad.4.vec_ref
  2.4 80.6 %shard_map.50 = (f32[512,256]{1,0:T(8,128)}, f32[16,2,16,256]{3,2,1,0:T(8,128)}) custom-call(bf16[2,256,1024]{2,1,0:T(8,128)(2,1)} %bitcast.3, bf16[1024,256]{1,0:T(8,128)(2,1)} %basis_ref.3, bf16[1024,256]{1,0:T(8,128)(2,1)} %pad.4.vec_ref), custom_call_target="tpu_custom_call" | custom-call | tf_op jit(solution)/shard_map/pallas_call | solution.py:719
  83.0 26.1 %shard_map.51 = (f32[256,256]{1,0:T(8,128)}, f32[512,256]{1,0:T(8,128)}) custom-call(f32[512,256]{1,0:T(8,128)} %get-tuple-element.6.s_ref), custom_call_target="tpu_custom_call" | custom-call | tf_op jit(solution)/shard_map/pallas_call | solution.py:102
  109.2 16.9 %shard_map.52.inv_ref = f32[256,256]{1,0:T(8,128)} custom-call(f32[256,256]{1,0:T(8,128)} %get-tuple-element.8.g_ref), custom_call_target="tpu_custom_call" | custom-call | tf_op jit(solution)/shard_map/pallas_call | solution.py:401
  126.1 1.3 constant_dynamic-slice_fusion.vec_ref
  127.4 114.7 %shard_map.53 = (f32[4,64]{1,0:T(4,128)}, f32[4,256]{1,0:T(4,128)}) custom-call(f32[512,256]{1,0:T(8,128)} %get-tuple-element.6.s_ref, f32[512,256]{1,0:T(8,128)} %get-tuple-element.7.next_ref, f32[256,256]{1,0:T(8,128)} %shard_map.52.inv_ref, f32[512,256]{1,0:T(8,128)} %bitcast.5, bf16[1024,256]{1,0:T(8,128)(2,1)} %basis_ref.3, ...), custom_call_target="tpu_custom_call" | custom-call | tf_op jit(solution)/shard_map/pallas_call | solution.py:319
  242.0 0.0 copy-start
  242.0 1.3 copy.8
  243.3 0.0 copy-done
  243.3 0.6 copy.9
Async XLA Ops:
  242.0 1.3 copy-start

commit v5 on v4

--- a/solution.py
+++ b/solution.py
@@ -41,85 +41,6 @@
         device_id=(section, row),
         device_id_type=MESH,
     )
-
-
-def gram_kernel(
-    ns, nr, s_ref, gram_ref, next_ref, part, got, red, rs_send, rs_recv, ag_send, ag_recv, n_send, n_recv
-):
-    s, r = lax.axis_index("section"), lax.axis_index("row")
-    rows = part.shape[0] // nr
-    barrier = pltpu.get_barrier_semaphore()
-    after, before = lax.rem(s + 1, ns), lax.rem(s + ns - 1, ns)
-    for step in range(1, nr):
-        pl.semaphore_signal(barrier, inc=1, device_id=(s, lax.rem(r + step, nr)), device_id_type=MESH)
-    pl.semaphore_signal(barrier, inc=1, device_id=(after, r), device_id_type=MESH)
-    pl.semaphore_signal(barrier, inc=1, device_id=(before, r), device_id_type=MESH)
-    sp = split(s_ref[...])
-    part[...] = dot3(sp, sp, TN)
-    pl.semaphore_wait(barrier, nr + 1)
-    shift = remote(s_ref, next_ref, n_send, n_recv, before, r)
-    shift.start()
-    scatter = []
-    for step in range(1, nr):
-        peer = lax.rem(r + step, nr)
-        cp = remote(
-            part.at[pl.ds(pl.multiple_of(peer * rows, rows), rows)],
-            got.at[step],
-            rs_send.at[step],
-            rs_recv.at[step],
-            s,
-            peer,
-        )
-        cp.start()
-        scatter.append(cp)
-    for cp in scatter:
-        cp.wait_recv()
-    total = part[pl.ds(pl.multiple_of(r * rows, rows), rows), :]
-    for step in range(1, nr):
-        total = total + got[step]
-    red[...] = total
-    mine = pl.ds(pl.multiple_of(r * rows, rows), rows)
-    gather = []
-    for step in range(1, nr):
-        peer = lax.rem(r + step, nr)
-        cp = remote(red, gram_ref.at[mine], ag_send.at[step], ag_recv.at[step], s, peer)
-        cp.start()
-        gather.append(cp)
-    gram_ref[mine, :] = total
-    for step in range(1, nr):
-        peer = lax.rem(r + nr - step, nr)
-        theirs = pl.ds(pl.multiple_of(peer * rows, rows), rows)
-        remote(red, gram_ref.at[theirs], ag_send.at[step], ag_recv.at[step], s, peer).wait_recv()
-    for cp in scatter + gather:
-        cp.wait_send()
-    shift.wait()
-
-
-def gram_call(sketch, ns, nr):
-    n = sketch.shape[1]
-    vm = pl.BlockSpec(memory_space=pltpu.VMEM)
-    dma = pltpu.SemaphoreType.DMA
-    return pl.pallas_call(
-        functools.partial(gram_kernel, ns, nr),
-        out_shape=(
-            jax.ShapeDtypeStruct((n, n), F32),
-            jax.ShapeDtypeStruct(sketch.shape, F32),
-        ),
-        in_specs=[vm],
-        out_specs=(vm, vm),
-        scratch_shapes=[
-            pltpu.VMEM((n, n), F32),
-            pltpu.VMEM((nr, n // nr, n), F32),
-            pltpu.VMEM((n // nr, n), F32),
-            dma((nr,)),
-            dma((nr,)),
-            dma((nr,)),
-            dma((nr,)),
-            dma,
-            dma,
-        ],
-        compiler_params=pltpu.CompilerParams(collective_id=0, has_side_effects=True),
-    )(sketch)
 
 
 def packed(c):
@@ -145,6 +66,8 @@
     coef_ref,
     hi_ref,
     lo_ref,
+    kept,
+    low_part,
     probe,
     moved,
     cout,
@@ -165,10 +88,14 @@
     s_recv,
     b_send,
     b_recv,
+    k_send,
+    k_recv,
 ):
     s, r = lax.axis_index("section"), lax.axis_index("row")
+    n = kept.shape[1]
+    odd = lax.rem(s, 2) == 1
     barrier = pltpu.get_barrier_semaphore()
-    after, before = lax.rem(s + 1, ns), lax.rem(s + ns - 1, ns)
+    after, before = lax.rem(s + 2, ns), lax.rem(s + ns - 2, ns)
     for q in range(nr):
         for other in (after, before):
             pl.semaphore_signal(barrier, inc=1, device_id=(other, q), device_id_type=MESH)
@@ -177,62 +104,78 @@
     for step in range(1, ns):
         pl.semaphore_signal(barrier, inc=1, device_id=(lax.rem(s + step, ns), r), device_id_type=MESH)
 
-    sp = split(s_ref[...])
-    nx = split(next_ref[...])
-    iv = split(inv_ref[...])
-    hi_ref[...], lo_ref[...] = split(dot3(iv, split(dot3(sp, nx, TN)), NN))
     pl.semaphore_wait(barrier, 3 * nr + ns - 2)
-
-    @pl.when(s == 0)
-    def _():
-        p = p0_ref[:, :128].T[:8]
-        probe[...] = p
-        cout[...] = packed(dot3(split(p), sp, NN))
-        copies = []
-        for step in range(1, nr):
-            peer = lax.rem(r + step, nr)
-            cp = remote(cout, cin.at[r], c_send.at[step], c_recv.at[r], 0, peer)
-            cp.start()
-            copies.append(cp)
-        cin[pl.ds(r, 1)] = cout[...][None]
-        for cp in copies:
-            cp.wait_send()
-        for step in range(1, nr):
-            peer = lax.rem(r + step, nr)
-            remote(cout, cin.at[peer], c_send.at[step], c_recv.at[peer], 0, peer).wait_recv()
-
-    @pl.when(s > 0)
-    def _():
-        remote(moved, probe, p_send, p_recv, before, r).wait_recv()
-
-    p = probe[...]
-    ahead = dot3(split(p), nx, NN)
-
-    @pl.when(s > 0)
-    def _():
-        for q in range(nr):
-            remote(cout, cin.at[q], c_send.at[q], c_recv.at[q], before, q).wait_recv()
-
-    total = cin[0]
-    for q in range(1, nr):
-        total = total + cin[q]
-    inner = unpacked(total)
-    cin_parts = split(inner)
-
-    @pl.when(s < ns - 1)
-    def _():
-        cout[...] = packed(ahead - dot3(cin_parts, (hi_ref[...], lo_ref[...]), NN))
-        for q in range(nr):
-            remote(cout, cin.at[r], c_send.at[q], c_recv.at[r], after, q).start()
-
-    coef = dot3(cin_parts, iv, NN)
-    cs = split(coef)
-    moved[...] = p - dot3(cs, sp, NT)
-
-    @pl.when(s < ns - 1)
-    def _():
-        remote(moved, probe, p_send, p_recv, after, r).start()
-
+    pass_coef = remote(low_part, kept, k_send, k_recv, lax.rem(s + ns - 1, ns), r)
+    take_coef = remote(low_part, kept, k_send, k_recv, lax.rem(s + 1, ns), r)
+
+    @pl.when(odd)
+    def _():
+        sp = split(s_ref[...])
+        nx = split(next_ref[...])
+        iv = split(inv_ref[...])
+
+        @pl.when(s == 1)
+        def _():
+            p = p0_ref[:, :128].T[:8]
+            probe[...] = p
+            cout[...] = packed(dot3(split(p), sp, NN))
+            copies = []
+            for step in range(1, nr):
+                peer = lax.rem(r + step, nr)
+                cp = remote(cout, cin.at[r], c_send.at[step], c_recv.at[r], 1, peer)
+                cp.start()
+                copies.append(cp)
+            cin[pl.ds(r, 1)] = cout[...][None]
+            for cp in copies:
+                cp.wait_send()
+
+        hi_ref[...], lo_ref[...] = split(dot3(iv, split(dot3(sp, nx, TN)), NN))
+
+        @pl.when(s == 1)
+        def _():
+            for step in range(1, nr):
+                peer = lax.rem(r + step, nr)
+                remote(cout, cin.at[peer], c_send.at[step], c_recv.at[peer], 1, peer).wait_recv()
+
+        @pl.when(s > 1)
+        def _():
+            remote(moved, probe, p_send, p_recv, before, r).wait_recv()
+
+        p = probe[...]
+        ahead = dot3(split(p), nx, NN)
+
+        @pl.when(s > 1)
+        def _():
+            for q in range(nr):
+                remote(cout, cin.at[q], c_send.at[q], c_recv.at[q], before, q).wait_recv()
+
+        total = cin[0]
+        for q in range(1, nr):
+            total = total + cin[q]
+        inner = split(unpacked(total))
+
+        @pl.when(s < ns - 1)
+        def _():
+            cout[...] = packed(ahead - dot3(inner, (hi_ref[...], lo_ref[...]), NN))
+            for q in range(nr):
+                remote(cout, cin.at[r], c_send.at[q], c_recv.at[r], after, q).start()
+
+        coef = dot3(inner, iv, NN)
+        low_part[...] = coef[:, :n]
+        kept[...] = coef[:, n:]
+        moved[...] = p - dot3(split(coef), sp, NT)
+
+        @pl.when(s < ns - 1)
+        def _():
+            remote(moved, probe, p_send, p_recv, after, r).start()
+
+        pass_coef.start()
+
+    @pl.when(lax.rem(s, 2) == 0)
+    def _():
+        take_coef.wait_recv()
+
+    coef = kept[...]
     coef_ref[...] = coef[:4]
     term = lax.dot_general(coef.astype(BF16), basis_ref[...], (NT, ((), ())), preferred_element_type=F32)
     for k in range(ns // 2):
@@ -286,9 +229,16 @@
     @pl.when(s < ns - 1)
     def _():
         remote(bout, bin_, b_send.at[0], b_recv, ns - 1, r).wait_recv()
+
+    @pl.when(odd & (s < ns - 1))
+    def _():
         for q in range(nr):
             remote(cout, cin.at[q], c_send.at[q], c_recv.at[q], after, q).wait_send()
         remote(moved, probe, p_send, p_recv, after, r).wait_send()
+
+    @pl.when(odd)
+    def _():
+        pass_coef.wait_send()
 
     small = bin_[...]
 
@@ -320,17 +270,19 @@
         functools.partial(chain_kernel, ns, nr),
         out_shape=(
             jax.ShapeDtypeStruct((4, mine.shape[1]), F32),
-            jax.ShapeDtypeStruct((4, n), F32),
+            jax.ShapeDtypeStruct((4, n // 2), F32),
         ),
         in_specs=[vm] * 6,
         out_specs=(vm, vm),
         scratch_shapes=[
             pltpu.VMEM((n, n), BF16),
             pltpu.VMEM((n, n), BF16),
+            pltpu.VMEM((8, n // 2), F32),
+            pltpu.VMEM((8, n // 2), F32),
             pltpu.VMEM((8, k), F32),
             pltpu.VMEM((8, k), F32),
-            pltpu.VMEM((8, 128), F32),
-            pltpu.VMEM((nr, 8, 128), F32),
+            pltpu.VMEM((8, n // 2), F32),
+            pltpu.VMEM((nr, 8, n // 2), F32),
             pltpu.VMEM((ns // 2, 8, 128), F32),
             pltpu.VMEM((ns, 8, 128), F32),
             pltpu.VMEM((8, 128), F32),
@@ -346,6 +298,8 @@
             dma((nr,)),
             dma((nr,)),
             dma((ns,)),
+            dma,
+            dma,
             dma,
         ],
         compiler_params=pltpu.CompilerParams(collective_id=1, has_side_effects=True),
@@ -373,37 +327,204 @@
     return a
 
 
-def inverse_kernel(g_ref, out_ref):
-    g = g_ref[...]
-    n = g.shape[0]
+def pair_kernel(
+    ns,
+    nr,
+    s_ref,
+    pair_ref,
+    ahead_ref,
+    uinv_ref,
+    part,
+    got,
+    red,
+    full,
+    inv,
+    mate_inv,
+    n_send,
+    n_recv,
+    rs_send,
+    rs_recv,
+    ag_send,
+    ag_recv,
+    i_send,
+    i_recv,
+):
+    s, r = lax.axis_index("section"), lax.axis_index("row")
+    n = s_ref.shape[1]
+    rows = n // nr
+    odd = lax.rem(s, 2) == 1
+    even = lax.rem(s, 2) == 0
+    barrier = pltpu.get_barrier_semaphore()
+    for step in range(1, nr):
+        pl.semaphore_signal(barrier, inc=1, device_id=(s, lax.rem(r + step, nr)), device_id_type=MESH)
+    for step in (1, 2, ns - 2, ns - 1):
+        pl.semaphore_signal(barrier, inc=1, device_id=(lax.rem(s + step, ns), r), device_id_type=MESH)
+
+    low, high = pl.ds(0, n), pl.ds(n, n)
+    to_mate = remote(s_ref, pair_ref.at[:, low], n_send.at[0], n_recv.at[0], lax.rem(s + 1, ns), r)
+    to_last = remote(s_ref, ahead_ref.at[:, low], n_send.at[1], n_recv.at[1], lax.rem(s + ns - 1, ns), r)
+    to_odd = remote(s_ref, ahead_ref.at[:, high], n_send.at[2], n_recv.at[2], lax.rem(s + ns - 2, ns), r)
+
+    def span(peer):
+        return pl.ds(pl.multiple_of(peer * rows, rows), rows)
+
+    def scatter(i, step):
+        peer = lax.rem(r + step, nr)
+        return remote(
+            part.at[i, span(peer)], got.at[i, step], rs_send.at[i, step], rs_recv.at[i, step], s, peer
+        )
+
+    def gather(i, step, sending):
+        peer = lax.rem(r + (step if sending else nr - step), nr)
+        where = span(r if sending else peer)
+        return remote(red.at[i], full.at[i, where], ag_send.at[i, step], ag_recv.at[i, step], s, peer)
+
+    def begin(i):
+        for step in range(1, nr):
+            scatter(i, step).start()
+
+    def middle(i):
+        for step in range(1, nr):
+            scatter(i, step).wait_recv()
+        total = part[i, span(r), :]
+        for step in range(1, nr):
+            total = total + got[i, step]
+        red[i] = total
+        for step in range(1, nr):
+            gather(i, step, True).start()
+        full[i, span(r), :] = total
+
+    def end(i):
+        for step in range(1, nr):
+            gather(i, step, False).wait_recv()
+        for step in range(1, nr):
+            scatter(i, step).wait_send()
+            gather(i, step, True).wait_send()
+
+    sp = split(s_ref[...])
+    part[0] = dot3(sp, sp, TN)
+    pl.semaphore_wait(barrier, nr + 3)
+    begin(0)
+
+    @pl.when(even)
+    def _():
+        to_mate.start()
+
+        @pl.when(s > 0)
+        def _():
+            to_last.start()
+
+    @pl.when(odd & (s > 1))
+    def _():
+        to_odd.start()
+
+    pair_ref[:, n:] = s_ref[...]
+    middle(0)
+
+    @pl.when(odd)
+    def _():
+        to_mate.wait_recv()
+        part[1] = dot3(split(pair_ref[:, :n]), sp, TN)
+        begin(1)
+
+    end(0)
+
+    def dot(x, y, dims):
+        return lax.dot_general(x, y, (dims, ((), ())), precision=HI, preferred_element_type=F32)
+
+    g = full[0]
     h = n // 2
     eye = lax.broadcasted_iota(jnp.int32, (n, n), 0) == lax.broadcasted_iota(jnp.int32, (n, n), 1)
     d = jnp.where(eye, g, 0.0)
     rs = lax.rsqrt(jnp.sum(d, axis=1, keepdims=True))
     cs = lax.rsqrt(jnp.sum(d, axis=0, keepdims=True))
     g = g * rs * cs
-
-    def dot(x, y, dims):
-        return lax.dot_general(x, y, (dims, ((), ())), precision=HI, preferred_element_type=F32)
-
     a, b, c = g[:h, :h], g[:h, h:], g[h:, h:]
     ai = eliminate(a)
     t = dot(ai, b, NN)
-    ci = eliminate(c - dot(b, t, TN))
+    rest = c - dot(b, t, TN)
+
+    @pl.when(odd)
+    def _():
+        middle(1)
+
+    ci = eliminate(rest)
     u = dot(t, ci, NN)
     top = jnp.concatenate([ai + dot(u, t, NT), -u], axis=1)
-    low = jnp.concatenate([-u.T, ci], axis=1)
-    out_ref[...] = jnp.concatenate([top, low], axis=0) * rs * cs
-
-
-def inverse(gram):
+    bottom = jnp.concatenate([-u.T, ci], axis=1)
+    inv[...] = jnp.concatenate([top, bottom], axis=0) * rs * cs
+    pass_inv = remote(inv, mate_inv, i_send, i_recv, lax.rem(s + 1, ns), r)
+
+    @pl.when(even)
+    def _():
+        pass_inv.start()
+
+    @pl.when(odd)
+    def _():
+        end(1)
+        mine = inv[...]
+        right = dot3(split(full[1]), split(mine), NN)
+        uinv_ref[n:, n:] = mine
+        uinv_ref[n:, :n] = jnp.zeros((n, n), F32)
+        pass_inv.wait_recv()
+        theirs = mate_inv[...]
+        uinv_ref[:n, :n] = theirs
+        uinv_ref[:n, n:] = -dot3(split(theirs), split(right), NN)
+
+        @pl.when(s < ns - 1)
+        def _():
+            to_last.wait_recv()
+            to_odd.wait_recv()
+
+        @pl.when(s == ns - 1)
+        def _():
+            ahead_ref[...] = jnp.zeros(ahead_ref.shape, F32)
+
+    @pl.when(even)
+    def _():
+        pass_inv.wait_send()
+        to_mate.wait_send()
+
+        @pl.when(s > 0)
+        def _():
+            to_last.wait_send()
+
+    @pl.when(odd & (s > 1))
+    def _():
+        to_odd.wait_send()
+
+
+def pair_call(sketch, ns, nr):
+    k, n = sketch.shape
     vm = pl.BlockSpec(memory_space=pltpu.VMEM)
+    dma = pltpu.SemaphoreType.DMA
     return pl.pallas_call(
-        inverse_kernel,
-        out_shape=jax.ShapeDtypeStruct(gram.shape, F32),
+        functools.partial(pair_kernel, ns, nr),
+        out_shape=(
+            jax.ShapeDtypeStruct((k, 2 * n), F32),
+            jax.ShapeDtypeStruct((k, 2 * n), F32),
+            jax.ShapeDtypeStruct((2 * n, 2 * n), F32),
+        ),
         in_specs=[vm],
-        out_specs=vm,
-    )(gram)
+        out_specs=(vm, vm, vm),
+        scratch_shapes=[
+            pltpu.VMEM((2, n, n), F32),
+            pltpu.VMEM((2, nr, n // nr, n), F32),
+            pltpu.VMEM((2, n // nr, n), F32),
+            pltpu.VMEM((2, n, n), F32),
+            pltpu.VMEM((n, n), F32),
+            pltpu.VMEM((n, n), F32),
+            dma((3,)),
+            dma((3,)),
+            dma((2, nr)),
+            dma((2, nr)),
+            dma((2, nr)),
+            dma((2, nr)),
+            dma,
+            dma,
+        ],
+        compiler_params=pltpu.CompilerParams(collective_id=0, has_side_effects=True),
+    )(sketch)
 
 
 def within(t, first, yes, no):
@@ -433,6 +554,7 @@
 
 
 UNITS = 34
+HOME = 1
 REACH = 4
 LAG = 3
 
@@ -492,14 +614,15 @@
     for row in (*beside, mate):
         hello(s, row)
 
-    @pl.when(s == 0)
-    def _():
-        for t in range(1, 16):
-            hello(t, r)
+    @pl.when(s == HOME)
+    def _():
+        for t in range(16):
+            if t != HOME:
+                hello(t, r)
 
     for cp in local:
         cp.wait()
-    pl.semaphore_wait(barrier, 8 + jnp.minimum(s, 1))
+    pl.semaphore_wait(barrier, 8 + jnp.where(s == HOME, 0, 1))
 
     def ocopy(src, dst, half, sem, dy):
         return remote(obuf.at[src, half], obuf.at[dst, half], o_send.at[sem], o_recv.at[sem], at(dy, 0), r)
@@ -546,7 +669,7 @@
         return remote(fbuf.at[u], s_ref.at[rows], f_send.at[u], f_recv.at[u], at(0, dx), r)
 
     def pcopy(u, sender):
-        return remote(fbuf.at[u], p_ref.at[sender, u], p_send.at[u], p_recv.at[sender, u], 0, r)
+        return remote(fbuf.at[u], p_ref.at[sender, u], p_send.at[u], p_recv.at[sender, u], HOME, r)
 
     def step(t, carry):
         done = t - 2 - LAG * REACH
@@ -573,11 +696,11 @@
 
         @pl.when((done >= 0) & (done < 2))
         def _():
-            @pl.when(s == 0)
+            @pl.when(s == HOME)
             def _():
-                p_ref[0, done] = fbuf[done]
-
-            @pl.when(s > 0)
+                p_ref[HOME, done] = fbuf[done]
+
+            @pl.when(s != HOME)
             def _():
                 pcopy(done, s).start()
 
@@ -677,13 +800,14 @@
 
     lax.fori_loop(2, UNITS, finish, 0)
 
-    @pl.when(s == 0)
-    def _():
-        for t in range(1, 16):
-            for u in range(2):
-                pcopy(u, t).wait_recv()
-
-    @pl.when(s > 0)
+    @pl.when(s == HOME)
+    def _():
+        for t in range(16):
+            if t != HOME:
+                for u in range(2):
+                    pcopy(u, t).wait_recv()
+
+    @pl.when(s != HOME)
     def _():
         for u in range(2):
             pcopy(u, s).wait_send()
@@ -754,11 +878,10 @@
     s = lax.axis_index("section")
     vecs = jnp.pad(vectors.T, ((0, 0), (0, basis.shape[1] - vectors.shape[0])))
     sketch, probe = sketch_call(omega, basis, vecs, nr)
-    gram, nxt = gram_call(sketch, ns, nr)
-    inv = inverse(gram)
+    pair, ahead, inv = pair_call(sketch, ns, nr)
     width = vectors.shape[1] // ns
     mine = lax.dynamic_slice_in_dim(vectors, s * width, width, 1)
-    return chain_call(sketch, nxt, inv, probe.reshape(-1, probe.shape[-1]), basis, mine, ns, nr)
+    return chain_call(pair, ahead, inv, probe.reshape(-1, probe.shape[-1]), basis, mine, ns, nr)
 
 
 def solution(mesh):

time: 244 us -> 221 us (0.906)
  Pallas kernels: 238 us -> 215 us
    pallas_call x1, Pallas kernels: 115 us -> 86 us  [chain_call(): pl.pallas_call(functools.partial(chain_kernel, ns, nr), out_shape=(jax.Sh...]
    pallas_call x2 -> x1, Pallas kernels: 43 us -> 48.6 us  [pair_call(): pl.pallas_call(functools.partial(pair_kernel, ns, nr), out_shape=(jax.Sha...]
where the time goes in v5:
time: 221 us; the launch traced here: 220 us
  Pallas kernels  215 us (97%)
  local copies, waits for them, and re-layouts  4.94 us (2%)
    pallas_call x1, Pallas kernels, chain_call(): pl.pallas_call(functools.partial(chain_kernel, ns, nr), out_shape=(jax.Sh...  86 us
    pallas_call x1, Pallas kernels, sketch_call(): pl.pallas_call(functools.partial(sketch_kernel, nz), out_shape=(jax.Shape...  80.1 us
    pallas_call x1, Pallas kernels, pair_call(): pl.pallas_call(functools.partial(pair_kernel, ns, nr), out_shape=(jax.Sha...  48.6 us

profile of v5, /device:TPU:1, one launch (start us, length us, event | category | flops | bytes accessed | tf_op | source)
XLA Modules:
  0.0 220.3 jit_solution(1262224337863467401)
XLA Ops:
  0.6 0.9 copy.5
  1.5 0.9 pad.4.vec_ref
  2.4 80.1 %shard_map.50 = (f32[512,256]{1,0:T(8,128)}, f32[16,2,16,256]{3,2,1,0:T(8,128)}) custom-call(bf16[2,256,1024]{2,1,0:T(8,128)(2,1)} %bitcast.3, bf16[1024,256]{1,0:T(8,128)(2,1)} %basis_ref.3, bf16[1024,256]{1,0:T(8,128)(2,1)} %pad.4.vec_ref), custom_call_target="tpu_custom_call" | custom-call | tf_op jit(solution)/shard_map/pallas_call | solution.py:843
  82.5 48.6 %shard_map.51 = (f32[512,512]{1,0:T(8,128)}, f32[512,512]{1,0:T(8,128)}, f32[512,512]{1,0:T(8,128)}) custom-call(f32[512,256]{1,0:T(8,128)} %get-tuple-element.7.s_ref), custom_call_target="tpu_custom_call" | custom-call | tf_op jit(solution)/shard_map/pallas_call | solution.py:501
  131.2 1.3 constant_dynamic-slice_fusion.vec_ref
  132.5 86.0 %shard_map.52 = (f32[4,64]{1,0:T(4,128)}, f32[4,256]{1,0:T(4,128)}) custom-call(f32[512,512]{1,0:T(8,128)} %get-tuple-element.8.s_ref, f32[512,512]{1,0:T(8,128)} %get-tuple-element.9.next_ref, f32[512,512]{1,0:T(8,128)} %get-tuple-element.10.inv_ref, f32[512,256]{1,0:T(8,128)} %bitcast.5, bf16[1024,256]{1,0:T(8,128)(2,1)} %basis_ref.3, ...), custom_call_target="tpu_custom_call" | custom-call | tf_op jit(solution)/shard_map/pallas_call | solution.py:269
  218.5 0.0 copy-start
  218.5 1.3 copy.8
  219.7 0.0 copy-done
  219.7 0.6 copy.9
Async XLA Ops:
  218.5 1.3 copy-start

commit v6 on v5

--- a/solution.py
+++ b/solution.py
@@ -90,25 +90,34 @@
     b_recv,
     k_send,
     k_recv,
+    dout,
+    din,
+    d_send,
+    d_recv,
 ):
     s, r = lax.axis_index("section"), lax.axis_index("row")
     n = kept.shape[1]
+    on = active(s)
+    off = jnp.logical_not(on)
     odd = lax.rem(s, 2) == 1
-    barrier = pltpu.get_barrier_semaphore()
-    after, before = lax.rem(s + 2, ns), lax.rem(s + ns - 2, ns)
-    for q in range(nr):
-        for other in (after, before):
-            pl.semaphore_signal(barrier, inc=1, device_id=(other, q), device_id_type=MESH)
-    for step in range(1, nr):
-        pl.semaphore_signal(barrier, inc=1, device_id=(s, lax.rem(r + step, nr)), device_id_type=MESH)
-    for step in range(1, ns):
-        pl.semaphore_signal(barrier, inc=1, device_id=(lax.rem(s + step, ns), r), device_id_type=MESH)
-
-    pl.semaphore_wait(barrier, 3 * nr + ns - 2)
-    pass_coef = remote(low_part, kept, k_send, k_recv, lax.rem(s + ns - 1, ns), r)
-    take_coef = remote(low_part, kept, k_send, k_recv, lax.rem(s + 1, ns), r)
-
-    @pl.when(odd)
+    mate = mate_of(s)
+    c = lax.rem(r, 2)
+    other_core = r + 1 - 2 * c
+    after, before = next_of(s, ns)
+
+    pass_coef = remote(low_part, kept, k_send, k_recv, mate, r)
+
+    def combine(i, value):
+        first, second = value[:, :128], value[:, 128:]
+        dout[i] = jnp.where(c == 0, second, first)
+        swap = remote(dout.at[i], din.at[i], d_send.at[i], d_recv.at[i], s, other_core)
+        swap.start()
+        keep = jnp.where(c == 0, first, second)
+        swap.wait_recv()
+        cout[...] = keep + din[i]
+        swap.wait_send()
+
+    @pl.when(on)
     def _():
         sp = split(s_ref[...])
         nx = split(next_ref[...])
@@ -116,9 +125,9 @@
 
         @pl.when(s == 1)
         def _():
-            p = p0_ref[:, :128].T[:8]
+            p = p0_ref[...].reshape(moved.shape[1], n)[:, :128].T[:8]
             probe[...] = p
-            cout[...] = packed(dot3(split(p), sp, NN))
+            combine(0, packed(dot3(split(p), sp, NN)))
             copies = []
             for step in range(1, nr):
                 peer = lax.rem(r + step, nr)
@@ -149,31 +158,31 @@
             for q in range(nr):
                 remote(cout, cin.at[q], c_send.at[q], c_recv.at[q], before, q).wait_recv()
 
-        total = cin[0]
-        for q in range(1, nr):
-            total = total + cin[q]
-        inner = split(unpacked(total))
-
-        @pl.when(s < ns - 1)
-        def _():
-            cout[...] = packed(ahead - dot3(inner, (hi_ref[...], lo_ref[...]), NN))
+        sums = [cin[0], cin[1]]
+        for q in range(2, nr):
+            sums[q % 2] = sums[q % 2] + cin[q]
+        inner = split(unpacked(jnp.concatenate(sums, axis=1)))
+
+        @pl.when(s != LAST)
+        def _():
+            combine(1, packed(ahead - dot3(inner, (hi_ref[...], lo_ref[...]), NN)))
             for q in range(nr):
                 remote(cout, cin.at[r], c_send.at[q], c_recv.at[r], after, q).start()
 
         coef = dot3(inner, iv, NN)
-        low_part[...] = coef[:, :n]
-        kept[...] = coef[:, n:]
+        low_part[...] = jnp.where(odd, coef[:, :n], coef[:, n:])
+        kept[...] = jnp.where(odd, coef[:, n:], coef[:, :n])
         moved[...] = p - dot3(split(coef), sp, NT)
 
-        @pl.when(s < ns - 1)
+        @pl.when(s != LAST)
         def _():
             remote(moved, probe, p_send, p_recv, after, r).start()
 
         pass_coef.start()
 
-    @pl.when(lax.rem(s, 2) == 0)
-    def _():
-        take_coef.wait_recv()
+    @pl.when(off)
+    def _():
+        pass_coef.wait_recv()
 
     coef = kept[...]
     coef_ref[...] = coef[:4]
@@ -188,7 +197,7 @@
         outs.append(cp)
     oin[pl.ds(s, 1)] = own[pl.ds(lax.div(s, 2), 1)]
 
-    @pl.when(s == ns - 1)
+    @pl.when(s == LAST)
     def _():
         m = split(moved[...])
         sq = dot3(m, m, NT)
@@ -208,10 +217,11 @@
             tot = tot + sin[q]
         bout[...] = tot
         bcs = []
-        for t in range(ns - 1):
-            cp = remote(bout, bin_, b_send.at[t], b_recv, t, r)
-            cp.start()
-            bcs.append(cp)
+        for t in range(ns):
+            if t != LAST:
+                cp = remote(bout, bin_, b_send.at[t], b_recv, t, r)
+                cp.start()
+                bcs.append(cp)
         for cp in copies + bcs:
             cp.wait_send()
         bin_[...] = tot
@@ -222,21 +232,21 @@
     removed = oin[0]
     for t in range(1, ns):
         removed = removed + oin[t]
-    odd = lax.rem(s, 2) == 1
-    removed = jnp.where(odd, removed[:4, 64:], removed[:4, :64])
-    remain = vec_ref[...].astype(F32) - removed
-
-    @pl.when(s < ns - 1)
-    def _():
-        remote(bout, bin_, b_send.at[0], b_recv, ns - 1, r).wait_recv()
-
-    @pl.when(odd & (s < ns - 1))
+    window = pl.ds(pl.multiple_of(lax.div(s, 2) * 128, 128), 128)
+    remain = vec_ref[:, window].astype(F32) - removed[:4]
+    remain = jnp.where(odd, remain[:, 64:], remain[:, :64])
+
+    @pl.when(s != LAST)
+    def _():
+        remote(bout, bin_, b_send.at[0], b_recv, LAST, r).wait_recv()
+
+    @pl.when(on & (s != LAST))
     def _():
         for q in range(nr):
             remote(cout, cin.at[q], c_send.at[q], c_recv.at[q], after, q).wait_send()
         remote(moved, probe, p_send, p_recv, after, r).wait_send()
 
-    @pl.when(odd)
+    @pl.when(on)
     def _():
         pass_coef.wait_send()
 
@@ -260,50 +270,6 @@
     ortho_ref[...] = jnp.concatenate(rows, axis=0)
     for cp in outs:
         cp.wait_send()
-
-
-def chain_call(sketch, nxt, inv, probe, basis, mine, ns, nr):
-    vm = pl.BlockSpec(memory_space=pltpu.VMEM)
-    dma = pltpu.SemaphoreType.DMA
-    k, n = sketch.shape
-    return pl.pallas_call(
-        functools.partial(chain_kernel, ns, nr),
-        out_shape=(
-            jax.ShapeDtypeStruct((4, mine.shape[1]), F32),
-            jax.ShapeDtypeStruct((4, n // 2), F32),
-        ),
-        in_specs=[vm] * 6,
-        out_specs=(vm, vm),
-        scratch_shapes=[
-            pltpu.VMEM((n, n), BF16),
-            pltpu.VMEM((n, n), BF16),
-            pltpu.VMEM((8, n // 2), F32),
-            pltpu.VMEM((8, n // 2), F32),
-            pltpu.VMEM((8, k), F32),
-            pltpu.VMEM((8, k), F32),
-            pltpu.VMEM((8, n // 2), F32),
-            pltpu.VMEM((nr, 8, n // 2), F32),
-            pltpu.VMEM((ns // 2, 8, 128), F32),
-            pltpu.VMEM((ns, 8, 128), F32),
-            pltpu.VMEM((8, 128), F32),
-            pltpu.VMEM((nr, 8, 128), F32),
-            pltpu.VMEM((8, 128), F32),
-            pltpu.VMEM((8, 128), F32),
-            dma((nr,)),
-            dma((nr,)),
-            dma,
-            dma,
-            dma((ns,)),
-            dma((ns,)),
-            dma((nr,)),
-            dma((nr,)),
-            dma((ns,)),
-            dma,
-            dma,
-            dma,
-        ],
-        compiler_params=pltpu.CompilerParams(collective_id=1, has_side_effects=True),
-    )(sketch, nxt, inv, probe, basis, mine)
 
 
 def eliminate(a):
@@ -327,9 +293,27 @@
     return a
 
 
+FIRST, LAST = 1, 14
+
+
+def active(s):
+    x = lax.rem(s, 4)
+    return (x == 1) | (x == 2)
+
+
+def mate_of(s):
+    return s + 1 - 2 * lax.rem(s, 2)
+
+
+def next_of(s, ns):
+    odd = lax.rem(s, 2) == 1
+    return lax.rem(s + jnp.where(odd, 1, 3), ns), lax.rem(s + ns - jnp.where(odd, 3, 1), ns)
+
+
 def pair_kernel(
     ns,
     nr,
+    close,
     s_ref,
     pair_ref,
     ahead_ref,
@@ -352,18 +336,22 @@
     s, r = lax.axis_index("section"), lax.axis_index("row")
     n = s_ref.shape[1]
     rows = n // nr
+    on = active(s)
+    off = jnp.logical_not(on)
     odd = lax.rem(s, 2) == 1
     even = lax.rem(s, 2) == 0
-    barrier = pltpu.get_barrier_semaphore()
-    for step in range(1, nr):
-        pl.semaphore_signal(barrier, inc=1, device_id=(s, lax.rem(r + step, nr)), device_id_type=MESH)
-    for step in (1, 2, ns - 2, ns - 1):
-        pl.semaphore_signal(barrier, inc=1, device_id=(lax.rem(s + step, ns), r), device_id_type=MESH)
-
+    mate = mate_of(s)
     low, high = pl.ds(0, n), pl.ds(n, n)
-    to_mate = remote(s_ref, pair_ref.at[:, low], n_send.at[0], n_recv.at[0], lax.rem(s + 1, ns), r)
-    to_last = remote(s_ref, ahead_ref.at[:, low], n_send.at[1], n_recv.at[1], lax.rem(s + ns - 1, ns), r)
-    to_odd = remote(s_ref, ahead_ref.at[:, high], n_send.at[2], n_recv.at[2], lax.rem(s + ns - 2, ns), r)
+    x = lax.rem(s, 4)
+    back = jnp.where(x == 1, 3, jnp.where(x == 2, 1, 2))
+    last = lax.rem(s + ns - back, ns)
+    to_mate = [
+        remote(s_ref, pair_ref.at[:, where], n_send.at[0], n_recv.at[0], mate, r) for where in (low, high)
+    ]
+    to_last = [
+        remote(s_ref, ahead_ref.at[:, where], n_send.at[1], n_recv.at[1 + k], last, r)
+        for k, where in enumerate((low, high))
+    ]
 
     def span(peer):
         return pl.ds(pl.multiple_of(peer * rows, rows), rows)
@@ -403,28 +391,34 @@
 
     sp = split(s_ref[...])
     part[0] = dot3(sp, sp, TN)
-    pl.semaphore_wait(barrier, nr + 3)
     begin(0)
-
-    @pl.when(even)
-    def _():
-        to_mate.start()
-
-        @pl.when(s > 0)
-        def _():
-            to_last.start()
-
-    @pl.when(odd & (s > 1))
-    def _():
-        to_odd.start()
-
-    pair_ref[:, n:] = s_ref[...]
+    close()
+
+    for k, mine in enumerate((even, odd)):
+
+        @pl.when(mine & off)
+        def _():
+            to_mate[k].start()
+
+        @pl.when(mine & (s >= 2))
+        def _():
+            to_last[k].start()
+
+        @pl.when(mine)
+        def _():
+            pair_ref[:, k * n : (k + 1) * n] = s_ref[...]
+
     middle(0)
 
-    @pl.when(odd)
-    def _():
-        to_mate.wait_recv()
-        part[1] = dot3(split(pair_ref[:, :n]), sp, TN)
+    for k, mine in enumerate((even, odd)):
+
+        @pl.when(mine & on)
+        def _():
+            to_mate[1 - k].wait_recv()
+
+    @pl.when(on)
+    def _():
+        part[1] = dot3(split(pair_ref[:, :n]), split(pair_ref[:, n:]), TN)
         begin(1)
 
     end(0)
@@ -444,7 +438,7 @@
     t = dot(ai, b, NN)
     rest = c - dot(b, t, TN)
 
-    @pl.when(odd)
+    @pl.when(on)
     def _():
         middle(1)
 
@@ -453,78 +447,54 @@
     top = jnp.concatenate([ai + dot(u, t, NT), -u], axis=1)
     bottom = jnp.concatenate([-u.T, ci], axis=1)
     inv[...] = jnp.concatenate([top, bottom], axis=0) * rs * cs
-    pass_inv = remote(inv, mate_inv, i_send, i_recv, lax.rem(s + 1, ns), r)
-
-    @pl.when(even)
+    pass_inv = remote(inv, mate_inv, i_send, i_recv, mate, r)
+
+    @pl.when(off)
     def _():
         pass_inv.start()
 
-    @pl.when(odd)
+    @pl.when(on)
     def _():
         end(1)
+        uinv_ref[n:, :n] = jnp.zeros((n, n), F32)
+
+    @pl.when(on & odd)
+    def _():
         mine = inv[...]
         right = dot3(split(full[1]), split(mine), NN)
         uinv_ref[n:, n:] = mine
-        uinv_ref[n:, :n] = jnp.zeros((n, n), F32)
         pass_inv.wait_recv()
         theirs = mate_inv[...]
         uinv_ref[:n, :n] = theirs
         uinv_ref[:n, n:] = -dot3(split(theirs), split(right), NN)
 
-        @pl.when(s < ns - 1)
-        def _():
-            to_last.wait_recv()
-            to_odd.wait_recv()
-
-        @pl.when(s == ns - 1)
-        def _():
-            ahead_ref[...] = jnp.zeros(ahead_ref.shape, F32)
-
-    @pl.when(even)
+    @pl.when(on & even)
+    def _():
+        mine = inv[...]
+        left = dot3(split(mine), split(full[1]), NN)
+        uinv_ref[:n, :n] = mine
+        pass_inv.wait_recv()
+        theirs = mate_inv[...]
+        uinv_ref[n:, n:] = theirs
+        uinv_ref[:n, n:] = -dot3(split(left), split(theirs), NN)
+
+    @pl.when(on & (s != LAST))
+    def _():
+        for cp in to_last:
+            cp.wait_recv()
+
+    @pl.when(s == LAST)
+    def _():
+        ahead_ref[...] = jnp.zeros(ahead_ref.shape, F32)
+
+    @pl.when(off)
     def _():
         pass_inv.wait_send()
-        to_mate.wait_send()
-
-        @pl.when(s > 0)
-        def _():
-            to_last.wait_send()
-
-    @pl.when(odd & (s > 1))
-    def _():
-        to_odd.wait_send()
-
-
-def pair_call(sketch, ns, nr):
-    k, n = sketch.shape
-    vm = pl.BlockSpec(memory_space=pltpu.VMEM)
-    dma = pltpu.SemaphoreType.DMA
-    return pl.pallas_call(
-        functools.partial(pair_kernel, ns, nr),
-        out_shape=(
-            jax.ShapeDtypeStruct((k, 2 * n), F32),
-            jax.ShapeDtypeStruct((k, 2 * n), F32),
-            jax.ShapeDtypeStruct((2 * n, 2 * n), F32),
-        ),
-        in_specs=[vm],
-        out_specs=(vm, vm, vm),
-        scratch_shapes=[
-            pltpu.VMEM((2, n, n), F32),
-            pltpu.VMEM((2, nr, n // nr, n), F32),
-            pltpu.VMEM((2, n // nr, n), F32),
-            pltpu.VMEM((2, n, n), F32),
-            pltpu.VMEM((n, n), F32),
-            pltpu.VMEM((n, n), F32),
-            dma((3,)),
-            dma((3,)),
-            dma((2, nr)),
-            dma((2, nr)),
-            dma((2, nr)),
-            dma((2, nr)),
-            dma,
-            dma,
-        ],
-        compiler_params=pltpu.CompilerParams(collective_id=0, has_side_effects=True),
-    )(sketch)
+        to_mate[0].wait_send()
+
+    @pl.when(s >= 2)
+    def _():
+        to_last[0].wait_send()
 
 
 def within(t, first, yes, no):
@@ -599,30 +569,32 @@
     local = [
         pltpu.make_async_copy(omega_ref, obuf.at[0], l_sem.at[0]),
         pltpu.make_async_copy(basis_ref, bbuf.at[0], l_sem.at[1]),
-        pltpu.make_async_copy(vec_ref, bbuf.at[4], l_sem.at[2]),
     ]
     for cp in local:
         cp.start()
 
     barrier = pltpu.get_barrier_semaphore()
+    ns, nr = 16, 2 * nz
 
     def hello(section, row):
         pl.semaphore_signal(barrier, inc=1, device_id=(section, row), device_id_type=MESH)
 
-    for dy, dx in ((1, 0), (3, 0), (0, 1), (0, 2), (0, 3)):
-        hello(at(dy, dx), r)
-    for row in (*beside, mate):
-        hello(s, row)
-
-    @pl.when(s == HOME)
-    def _():
-        for t in range(16):
-            if t != HOME:
-                hello(t, r)
-
+    for q in range(nr):
+        for other in next_of(s, ns):
+            hello(other, q)
+    for step in range(1, nr):
+        hello(s, lax.rem(r + step, nr))
+    for step in range(1, ns):
+        hello(lax.rem(s + step, ns), r)
+
+    v = vec_ref[...].astype(F32)
+    v = jnp.concatenate([v, jnp.zeros_like(v)], axis=0)
+    v = jnp.concatenate([v, jnp.zeros((120, v.shape[1]), F32)], axis=0)
+    bbuf[4, :, :128] = v.T.astype(BF16)
+    bbuf[4, :, 128:] = jnp.zeros((v.shape[1], bbuf.shape[2] - 128), BF16)
     for cp in local:
         cp.wait()
-    pl.semaphore_wait(barrier, 8 + jnp.where(s == HOME, 0, 1))
+    pl.semaphore_wait(barrier, 3 * nr + ns - 2)
 
     def ocopy(src, dst, half, sem, dy):
         return remote(obuf.at[src, half], obuf.at[dst, half], o_send.at[sem], o_recv.at[sem], at(dy, 0), r)
@@ -794,7 +766,7 @@
 
         @pl.when(dx > 0)
         def _():
-            fcopy(u).wait()
+            fcopy(u).wait_recv()
 
         return carry
 
@@ -807,16 +779,14 @@
                 for u in range(2):
                     pcopy(u, t).wait_recv()
 
-    @pl.when(s != HOME)
-    def _():
-        for u in range(2):
-            pcopy(u, s).wait_send()
-
-    for cp in b_own + o_own + o_rest + b_fwd + o_fwd:
-        cp.wait_send()
-
     def drain(u, carry):
         dcopy(u).wait_send()
+        dx, _ = place(u)
+
+        @pl.when((u >= 2) & (dx > 0))
+        def _():
+            fcopy(u).wait_send()
+
         for d in range(2):
             for k in range(REACH):
                 if k:
@@ -829,59 +799,154 @@
 
         return carry
 
-    lax.fori_loop(0, UNITS, drain, 0)
-
-
-def sketch_call(omega, basis, vecs, nr):
+    def close():
+        @pl.when(s != HOME)
+        def _():
+            for u in range(2):
+                pcopy(u, s).wait_send()
+
+        for cp in b_own + o_own + o_rest + b_fwd + o_fwd:
+            cp.wait_send()
+        lax.fori_loop(0, UNITS, drain, 0)
+
+    return close
+
+
+def sketch_scratch(m, k, n, nr):
+    nz, piece, dma = nr // 2, m // nr // 2, pltpu.SemaphoreType.DMA
+    return [
+        pltpu.VMEM((4, 2, m // 2, k), BF16),
+        pltpu.VMEM((5, k, n), BF16),
+        pltpu.VMEM((UNITS, nz, 2, piece, n), F32),
+        pltpu.VMEM((UNITS, nz, piece, n), F32),
+        pltpu.VMEM((UNITS, 2, REACH, piece, n), F32),
+        pltpu.VMEM((UNITS, piece, n), F32),
+        dma((2,)),
+        dma((6,)),
+        dma((6,)),
+        dma((4,)),
+        dma((4,)),
+        dma((UNITS,)),
+        dma((UNITS,)),
+        dma((UNITS, 2, REACH)),
+        dma((UNITS, 2, REACH)),
+        dma((UNITS,)),
+        dma((UNITS,)),
+        dma((2,)),
+        dma((16, 2)),
+    ]
+
+
+def pair_scratch(n, nr):
+    dma = pltpu.SemaphoreType.DMA
+    return [
+        pltpu.VMEM((2, n, n), F32),
+        pltpu.VMEM((2, nr, n // nr, n), F32),
+        pltpu.VMEM((2, n // nr, n), F32),
+        pltpu.VMEM((2, n, n), F32),
+        pltpu.VMEM((n, n), F32),
+        pltpu.VMEM((n, n), F32),
+        dma((3,)),
+        dma((3,)),
+        dma((2, nr)),
+        dma((2, nr)),
+        dma((2, nr)),
+        dma((2, nr)),
+        dma,
+        dma,
+    ]
+
+
+def chain_scratch(k, n, ns, nr):
+    dma = pltpu.SemaphoreType.DMA
+    return [
+        pltpu.VMEM((n, n), BF16),
+        pltpu.VMEM((n, n), BF16),
+        pltpu.VMEM((8, n // 2), F32),
+        pltpu.VMEM((8, n // 2), F32),
+        pltpu.VMEM((8, k), F32),
+        pltpu.VMEM((8, k), F32),
+        pltpu.VMEM((8, 128), F32),
+        pltpu.VMEM((nr, 8, 128), F32),
+        pltpu.VMEM((ns // 2, 8, 128), F32),
+        pltpu.VMEM((ns, 8, 128), F32),
+        pltpu.VMEM((8, 128), F32),
+        pltpu.VMEM((nr, 8, 128), F32),
+        pltpu.VMEM((8, 128), F32),
+        pltpu.VMEM((8, 128), F32),
+        dma((nr,)),
+        dma((nr,)),
+        dma,
+        dma,
+        dma((ns,)),
+        dma((ns,)),
+        dma((nr,)),
+        dma((nr,)),
+        dma((ns,)),
+        dma,
+        dma,
+        dma,
+        pltpu.VMEM((2, 8, 128), F32),
+        pltpu.VMEM((2, 8, 128), F32),
+        dma((2,)),
+        dma((2,)),
+    ]
+
+
+def whole_kernel(ns, nr, ends, omega_ref, basis_ref, vec_ref, ortho_ref, coef_ref, *rest):
+    s_ref, p_ref, pair_ref, ahead_ref, uinv_ref = rest[:5]
+    first, second = rest[5 : ends[0]], rest[ends[0] : ends[1]]
+    close = sketch_kernel(nr // 2, omega_ref, basis_ref, vec_ref, s_ref, p_ref, *first)
+    pair_kernel(ns, nr, close, s_ref, pair_ref, ahead_ref, uinv_ref, *second)
+    own_basis = first[1].at[0]
+    chain_kernel(
+        ns,
+        nr,
+        pair_ref,
+        ahead_ref,
+        uinv_ref,
+        p_ref,
+        own_basis,
+        vec_ref,
+        ortho_ref,
+        coef_ref,
+        *rest[ends[1] :],
+    )
+
+
+def whole_call(omega, basis, vectors, ns, nr):
     vm = pl.BlockSpec(memory_space=pltpu.VMEM)
     anym = pl.BlockSpec(memory_space=pl.ANY)
-    dma = pltpu.SemaphoreType.DMA
-    nz = nr // 2
     m, k = omega.shape
     n = basis.shape[1]
-    piece = m // nr // 2
+    kept = [
+        pltpu.VMEM((m, n), F32),
+        pltpu.VMEM((ns, 2, m // nr // 2, n), F32),
+        pltpu.VMEM((m, 2 * n), F32),
+        pltpu.VMEM((m, 2 * n), F32),
+        pltpu.VMEM((2 * n, 2 * n), F32),
+    ]
+    one = sketch_scratch(m, k, n, nr)
+    two = pair_scratch(n, nr)
+    three = chain_scratch(m, 2 * n, ns, nr)
+    ends = (len(kept) + len(one), len(kept) + len(one) + len(two))
     return pl.pallas_call(
-        functools.partial(sketch_kernel, nz),
+        functools.partial(whole_kernel, ns, nr, ends),
         out_shape=(
-            jax.ShapeDtypeStruct((m, n), F32),
-            jax.ShapeDtypeStruct((16, 2, piece, n), F32),
+            jax.ShapeDtypeStruct((4, vectors.shape[1] // ns), F32),
+            jax.ShapeDtypeStruct((4, n), F32),
         ),
-        in_specs=[anym] * 3,
+        in_specs=[anym, anym, vm],
         out_specs=(vm, vm),
-        scratch_shapes=[
-            pltpu.VMEM((4, 2, m // 2, k), BF16),
-            pltpu.VMEM((5, k, n), BF16),
-            pltpu.VMEM((UNITS, nz, 2, piece, n), F32),
-            pltpu.VMEM((UNITS, nz, piece, n), F32),
-            pltpu.VMEM((UNITS, 2, REACH, piece, n), F32),
-            pltpu.VMEM((UNITS, piece, n), F32),
-            dma((3,)),
-            dma((6,)),
-            dma((6,)),
-            dma((4,)),
-            dma((4,)),
-            dma((UNITS,)),
-            dma((UNITS,)),
-            dma((UNITS, 2, REACH)),
-            dma((UNITS, 2, REACH)),
-            dma((UNITS,)),
-            dma((UNITS,)),
-            dma((2,)),
-            dma((16, 2)),
-        ],
-        compiler_params=pltpu.CompilerParams(collective_id=2, has_side_effects=True),
-    )(omega.reshape(2, m // 2, k), basis, vecs)
+        scratch_shapes=kept + one + two + three,
+        compiler_params=pltpu.CompilerParams(
+            collective_id=0, has_side_effects=True, vmem_limit_bytes=60 * 1024 * 1024
+        ),
+    )(omega.reshape(2, m // 2, k), basis, vectors)
 
 
 def body(omega, basis, vectors):
-    ns, nr = lax.axis_size("section"), lax.axis_size("row")
-    s = lax.axis_index("section")
-    vecs = jnp.pad(vectors.T, ((0, 0), (0, basis.shape[1] - vectors.shape[0])))
-    sketch, probe = sketch_call(omega, basis, vecs, nr)
-    pair, ahead, inv = pair_call(sketch, ns, nr)
-    width = vectors.shape[1] // ns
-    mine = lax.dynamic_slice_in_dim(vectors, s * width, width, 1)
-    return chain_call(pair, ahead, inv, probe.reshape(-1, probe.shape[-1]), basis, mine, ns, nr)
+    return whole_call(omega, basis, vectors, lax.axis_size("section"), lax.axis_size("row"))
 
 
 def solution(mesh):

time: 221 us -> 199 us (0.900)
  Pallas kernels: 215 us -> 196 us
  local copies, waits for them, and re-layouts: 4.94 us -> 1.84 us
    pallas_call x3 -> x1, Pallas kernels: 215 us -> 196 us  [whole_call(): pl.pallas_call(functools.partial(whole_kernel, ns, nr, ends), out_shape=(...]
where the time goes in v6:
time: 199 us; the launch traced here: 198 us
  Pallas kernels  196 us (98%)
    pallas_call x1, Pallas kernels, whole_call(): pl.pallas_call(functools.partial(whole_kernel, ns, nr, ends), out_shape=(...  196 us

profile of v6, /device:TPU:1, one launch (start us, length us, event | category | flops | bytes accessed | tf_op | source)
XLA Modules:
  0.0 198.5 jit_solution(14304041972847984041)
XLA Ops:
  0.6 196.0 %shard_map.50 = (f32[4,64]{1,0:T(4,128)}, f32[4,256]{1,0:T(4,128)}) custom-call(bf16[2,256,1024]{2,1,0:T(8,128)(2,1)} %bitcast.1, bf16[1024,256]{1,0:T(8,128)(2,1)} %basis_ref.1, bf16[4,1024]{1,0:T(4,128)(2,1)} %vec_ref.1), custom_call_target="tpu_custom_call" | custom-call | tf_op jit(solution)/shard_map/pallas_call | solution.py:933
  196.6 0.0 copy-start
  196.6 1.2 copy.7
  197.9 0.0 copy-done
  197.9 0.6 copy.8
Async XLA Ops:
  196.6 1.3 copy-start

commit v7 on v6

--- a/solution.py
+++ b/solution.py
@@ -53,13 +53,38 @@
     return jnp.concatenate([wide, jnp.zeros_like(wide)], axis=0)
 
 
+def combine(i, value, cout, dout, din, d_send, d_recv):
+    s, r = lax.axis_index("section"), lax.axis_index("row")
+    c = lax.rem(r, 2)
+    first, second = value[:, :128], value[:, 128:]
+    dout[i] = jnp.where(c == 0, second, first)
+    swap = remote(dout.at[i], din.at[i], d_send.at[i], d_recv.at[i], s, r + 1 - 2 * c)
+    swap.start()
+    keep = jnp.where(c == 0, first, second)
+    swap.wait_recv()
+    cout[...] = keep + din[i]
+    swap.wait_send()
+
+
+def first_products(nr, s_ref, p0_ref, refs):
+    probe, cout, cin, c_send, c_recv = refs[4], refs[6], refs[7], refs[14], refs[15]
+    r = lax.axis_index("row")
+    rows, n = s_ref.shape
+    p = p0_ref[...].reshape(rows, n // 2)[:, :128].T[:8]
+    probe[...] = p
+    combine(0, packed(dot3(split(p), split(s_ref[...]), NN)), cout, *refs[-4:])
+    for step in range(1, nr):
+        remote(cout, cin.at[r], c_send.at[step], c_recv.at[r], FIRST, lax.rem(r + step, nr)).start()
+    cin[pl.ds(r, 1)] = cout[...][None]
+
+
 def chain_kernel(
     ns,
     nr,
     s_ref,
     next_ref,
     inv_ref,
-    p0_ref,
+    cross_ref,
     basis_ref,
     vec_ref,
     ortho_ref,
@@ -101,21 +126,9 @@
     off = jnp.logical_not(on)
     odd = lax.rem(s, 2) == 1
     mate = mate_of(s)
-    c = lax.rem(r, 2)
-    other_core = r + 1 - 2 * c
     after, before = next_of(s, ns)
 
     pass_coef = remote(low_part, kept, k_send, k_recv, mate, r)
-
-    def combine(i, value):
-        first, second = value[:, :128], value[:, 128:]
-        dout[i] = jnp.where(c == 0, second, first)
-        swap = remote(dout.at[i], din.at[i], d_send.at[i], d_recv.at[i], s, other_core)
-        swap.start()
-        keep = jnp.where(c == 0, first, second)
-        swap.wait_recv()
-        cout[...] = keep + din[i]
-        swap.wait_send()
 
     @pl.when(on)
     def _():
@@ -123,37 +136,22 @@
         nx = split(next_ref[...])
         iv = split(inv_ref[...])
 
-        @pl.when(s == 1)
-        def _():
-            p = p0_ref[...].reshape(moved.shape[1], n)[:, :128].T[:8]
-            probe[...] = p
-            combine(0, packed(dot3(split(p), sp, NN)))
-            copies = []
+        hi_ref[...], lo_ref[...] = split(dot3(iv, split(cross_ref[...]), NN))
+
+        @pl.when(s == FIRST)
+        def _():
             for step in range(1, nr):
                 peer = lax.rem(r + step, nr)
-                cp = remote(cout, cin.at[r], c_send.at[step], c_recv.at[r], 1, peer)
-                cp.start()
-                copies.append(cp)
-            cin[pl.ds(r, 1)] = cout[...][None]
-            for cp in copies:
-                cp.wait_send()
-
-        hi_ref[...], lo_ref[...] = split(dot3(iv, split(dot3(sp, nx, TN)), NN))
-
-        @pl.when(s == 1)
-        def _():
-            for step in range(1, nr):
-                peer = lax.rem(r + step, nr)
-                remote(cout, cin.at[peer], c_send.at[step], c_recv.at[peer], 1, peer).wait_recv()
-
-        @pl.when(s > 1)
+                remote(cout, cin.at[peer], c_send.at[step], c_recv.at[peer], FIRST, peer).wait()
+
+        @pl.when(s != FIRST)
         def _():
             remote(moved, probe, p_send, p_recv, before, r).wait_recv()
 
         p = probe[...]
         ahead = dot3(split(p), nx, NN)
 
-        @pl.when(s > 1)
+        @pl.when(s != FIRST)
         def _():
             for q in range(nr):
                 remote(cout, cin.at[q], c_send.at[q], c_recv.at[q], before, q).wait_recv()
@@ -165,7 +163,8 @@
 
         @pl.when(s != LAST)
         def _():
-            combine(1, packed(ahead - dot3(inner, (hi_ref[...], lo_ref[...]), NN)))
+            partial = packed(ahead - dot3(inner, (hi_ref[...], lo_ref[...]), NN))
+            combine(1, partial, cout, dout, din, d_send, d_recv)
             for q in range(nr):
                 remote(cout, cin.at[r], c_send.at[q], c_recv.at[r], after, q).start()
 
@@ -314,16 +313,21 @@
     ns,
     nr,
     close,
+    start_chain,
     s_ref,
     pair_ref,
     ahead_ref,
     uinv_ref,
+    cross_ref,
     part,
     got,
     red,
     full,
     inv,
-    mate_inv,
+    early,
+    late,
+    mate_early,
+    mate_late,
     n_send,
     n_recv,
     rs_send,
@@ -437,59 +441,77 @@
     ai = eliminate(a)
     t = dot(ai, b, NN)
     rest = c - dot(b, t, TN)
+    early[0] = ai * rs[:h] * cs[:, :h]
+    early[1] = t * rs[:h] / cs[:, h:]
+    pass_early = remote(early, mate_early, i_send.at[0], i_recv.at[0], mate, r)
+    pass_late = remote(late, mate_late, i_send.at[1], i_recv.at[1], mate, r)
+
+    @pl.when(off)
+    def _():
+        pass_early.start()
 
     @pl.when(on)
     def _():
         middle(1)
 
-    ci = eliminate(rest)
-    u = dot(t, ci, NN)
-    top = jnp.concatenate([ai + dot(u, t, NT), -u], axis=1)
-    bottom = jnp.concatenate([-u.T, ci], axis=1)
-    inv[...] = jnp.concatenate([top, bottom], axis=0) * rs * cs
-    pass_inv = remote(inv, mate_inv, i_send, i_recv, mate, r)
+    @pl.when(s == FIRST)
+    def _():
+        start_chain()
+
+    late[...] = eliminate(rest) * rs[h:] * cs[:, h:]
 
     @pl.when(off)
     def _():
-        pass_inv.start()
+        pass_late.start()
+
+    def whole_inverse(parts, corner):
+        t, ci = parts[1], corner[...]
+        u = dot(t, ci, NN)
+        top = jnp.concatenate([parts[0] + dot(u, t, NT), -u], axis=1)
+        bottom = jnp.concatenate([-u.T, ci], axis=1)
+        return jnp.concatenate([top, bottom], axis=0)
 
     @pl.when(on)
     def _():
+        inv[...] = whole_inverse(early, late)
+        uinv_ref[n:, :n] = jnp.zeros((n, n), F32)
+
+    @pl.when(on & (s != LAST))
+    def _():
+        for cp in to_last:
+            cp.wait_recv()
+
+    @pl.when(s == LAST)
+    def _():
+        ahead_ref[...] = jnp.zeros(ahead_ref.shape, F32)
+
+    @pl.when(on)
+    def _():
+        cross_ref[...] = dot3(split(pair_ref[...]), split(ahead_ref[...]), TN)
         end(1)
-        uinv_ref[n:, :n] = jnp.zeros((n, n), F32)
+        pass_early.wait_recv()
+        pass_late.wait_recv()
 
     @pl.when(on & odd)
     def _():
-        mine = inv[...]
+        mine, theirs = inv[...], whole_inverse(mate_early, mate_late)
         right = dot3(split(full[1]), split(mine), NN)
         uinv_ref[n:, n:] = mine
-        pass_inv.wait_recv()
-        theirs = mate_inv[...]
         uinv_ref[:n, :n] = theirs
         uinv_ref[:n, n:] = -dot3(split(theirs), split(right), NN)
 
     @pl.when(on & even)
     def _():
-        mine = inv[...]
+        mine, theirs = inv[...], whole_inverse(mate_early, mate_late)
         left = dot3(split(mine), split(full[1]), NN)
         uinv_ref[:n, :n] = mine
-        pass_inv.wait_recv()
-        theirs = mate_inv[...]
         uinv_ref[n:, n:] = theirs
         uinv_ref[:n, n:] = -dot3(split(left), split(theirs), NN)
 
-    @pl.when(on & (s != LAST))
-    def _():
-        for cp in to_last:
-            cp.wait_recv()
-
-    @pl.when(s == LAST)
-    def _():
-        ahead_ref[...] = jnp.zeros(ahead_ref.shape, F32)
-
     @pl.when(off)
     def _():
-        pass_inv.wait_send()
+        pass_early.wait_send()
+        pass_late.wait_send()
         to_mate[0].wait_send()
 
     @pl.when(s >= 2)
@@ -845,15 +867,18 @@
         pltpu.VMEM((2, n // nr, n), F32),
         pltpu.VMEM((2, n, n), F32),
         pltpu.VMEM((n, n), F32),
-        pltpu.VMEM((n, n), F32),
+        pltpu.VMEM((2, n // 2, n // 2), F32),
+        pltpu.VMEM((n // 2, n // 2), F32),
+        pltpu.VMEM((2, n // 2, n // 2), F32),
+        pltpu.VMEM((n // 2, n // 2), F32),
         dma((3,)),
         dma((3,)),
         dma((2, nr)),
         dma((2, nr)),
         dma((2, nr)),
         dma((2, nr)),
-        dma,
-        dma,
+        dma((2,)),
+        dma((2,)),
     ]
 
 
@@ -894,10 +919,17 @@
 
 
 def whole_kernel(ns, nr, ends, omega_ref, basis_ref, vec_ref, ortho_ref, coef_ref, *rest):
-    s_ref, p_ref, pair_ref, ahead_ref, uinv_ref = rest[:5]
-    first, second = rest[5 : ends[0]], rest[ends[0] : ends[1]]
+    s_ref, p_ref, pair_ref, ahead_ref, uinv_ref, cross_ref = rest[:6]
+    first, second = rest[6 : ends[0]], rest[ends[0] : ends[1]]
+    third = rest[ends[1] :]
     close = sketch_kernel(nr // 2, omega_ref, basis_ref, vec_ref, s_ref, p_ref, *first)
-    pair_kernel(ns, nr, close, s_ref, pair_ref, ahead_ref, uinv_ref, *second)
+
+    def start_chain():
+        first_products(nr, pair_ref, p_ref, third)
+
+    pair_kernel(
+        ns, nr, close, start_chain, s_ref, pair_ref, ahead_ref, uinv_ref, cross_ref, *second
+    )
     own_basis = first[1].at[0]
     chain_kernel(
         ns,
@@ -905,12 +937,12 @@
         pair_ref,
         ahead_ref,
         uinv_ref,
-        p_ref,
+        cross_ref,
         own_basis,
         vec_ref,
         ortho_ref,
         coef_ref,
-        *rest[ends[1] :],
+        *third,
     )
 
 
@@ -924,6 +956,7 @@
         pltpu.VMEM((ns, 2, m // nr // 2, n), F32),
         pltpu.VMEM((m, 2 * n), F32),
         pltpu.VMEM((m, 2 * n), F32),
+        pltpu.VMEM((2 * n, 2 * n), F32),
         pltpu.VMEM((2 * n, 2 * n), F32),
     ]
     one = sketch_scratch(m, k, n, nr)

time: 199 us -> 190 us (0.955)
  Pallas kernels: 196 us -> 188 us
    pallas_call x1, Pallas kernels: 196 us -> 188 us  [whole_call(): pl.pallas_call(functools.partial(whole_kernel, ns, nr, ends), out_shape=(...]
where the time goes in v7:
time: 190 us
  Pallas kernels  188 us (99%)
    pallas_call x1, Pallas kernels, whole_call(): pl.pallas_call(functools.partial(whole_kernel, ns, nr, ends), out_shape=(...  188 us

profile of v7, /device:TPU:1, one launch (start us, length us, event | category | flops | bytes accessed | tf_op | source)
XLA Modules:
  0.0 190.1 jit_solution(12593156518860742161)
XLA Ops:
  0.6 187.6 %shard_map.50 = (f32[4,64]{1,0:T(4,128)}, f32[4,256]{1,0:T(4,128)}) custom-call(bf16[2,256,1024]{2,1,0:T(8,128)(2,1)} %bitcast.1, bf16[1024,256]{1,0:T(8,128)(2,1)} %basis_ref.1, bf16[4,1024]{1,0:T(4,128)(2,1)} %vec_ref.1), custom_call_target="tpu_custom_call" | custom-call | tf_op jit(solution)/shard_map/pallas_call | solution.py:966
  188.3 0.0 copy-start
  188.3 1.2 copy.7
  189.5 0.0 copy-done
  189.5 0.6 copy.8
Async XLA Ops:
  188.3 1.3 copy-start

commit v8 on v7

--- a/solution.py
+++ b/solution.py
@@ -273,22 +273,40 @@
 
 def eliminate(a):
     n = a.shape[0]
-    rows = lax.broadcasted_iota(jnp.int32, (n, n), 0)
     cols = lax.broadcasted_iota(jnp.int32, (n, n), 1)
     lane = lax.broadcasted_iota(jnp.int32, (1, n), 1)
-    for k in range(0, n, 2):
-        c1 = jnp.broadcast_to(a[:, k : k + 1], (n, n))
-        c2 = jnp.broadcast_to(a[:, k + 1 : k + 2], (n, n))
-        p, q, s = c1[k : k + 1], c2[k : k + 1], c2[k + 1 : k + 2]
-        e = 1.0 / (p * s - q * q)
-        r1 = jnp.where(lane == k, 1.0, jnp.where(lane == k + 1, 0.0, a[k : k + 1, :]))
-        r2 = jnp.where(lane == k + 1, 1.0, jnp.where(lane == k, 0.0, a[k + 1 : k + 2, :]))
-        w1 = (s * e) * r1 - (q * e) * r2
-        w2 = (p * e) * r2 - (q * e) * r1
-        base = jnp.where((cols == k) | (cols == k + 1), 0.0, a)
-        new = base - c1 * w1 - c2 * w2
-        last = jnp.where(rows == k + 1, jnp.broadcast_to(w2, (n, n)), new)
-        a = jnp.where(rows == k, jnp.broadcast_to(w1, (n, n)), last)
+    sub = lax.broadcasted_iota(jnp.int32, (8, n), 0)
+    for k in range(0, n, 4):
+        c = [jnp.broadcast_to(a[:, k + i : k + i + 1], (n, n)) for i in range(4)]
+        b = [[c[j][k + i : k + i + 1] for j in range(4)] for i in range(4)]
+        inside = (lane >= k) & (lane < k + 4)
+        r = [
+            jnp.where(lane == k + i, 1.0, jnp.where(inside, 0.0, a[k + i : k + i + 1, :])) for i in range(4)
+        ]
+        e = 1.0 / (b[0][0] * b[1][1] - b[0][1] * b[0][1])
+        a00, a01, a11 = b[1][1] * e, -b[0][1] * e, b[0][0] * e
+        f00 = a00 * b[0][2] + a01 * b[1][2]
+        f01 = a00 * b[0][3] + a01 * b[1][3]
+        f10 = a01 * b[0][2] + a11 * b[1][2]
+        f11 = a01 * b[0][3] + a11 * b[1][3]
+        s00 = b[2][2] - (b[0][2] * f00 + b[1][2] * f10)
+        s01 = b[2][3] - (b[0][2] * f01 + b[1][2] * f11)
+        s11 = b[3][3] - (b[0][3] * f01 + b[1][3] * f11)
+        g = 1.0 / (s00 * s11 - s01 * s01)
+        z2 = r[2] - (f00 * r[0] + f10 * r[1])
+        z3 = r[3] - (f01 * r[0] + f11 * r[1])
+        w2 = g * (s11 * z2 - s01 * z3)
+        w3 = g * (s00 * z3 - s01 * z2)
+        w0 = (a00 * r[0] + a01 * r[1]) - (f00 * w2 + f01 * w3)
+        w1 = (a01 * r[0] + a11 * r[1]) - (f10 * w2 + f11 * w3)
+        base = jnp.where((cols >= k) & (cols < k + 4), 0.0, a)
+        new = ((base - c[0] * w0) - c[1] * w1) - (c[2] * w2 + c[3] * w3)
+        at = k // 8 * 8
+        group = new[at : at + 8]
+        for i, w in enumerate((w0, w1, w2, w3)):
+            group = jnp.where(sub == k - at + i, jnp.broadcast_to(w, (8, n)), group)
+        pieces = [new[:at], group, new[at + 8 :]]
+        a = jnp.concatenate([p for p in pieces if p.shape[0]], axis=0)
     return a
 
 
@@ -548,7 +566,7 @@
 UNITS = 34
 HOME = 1
 REACH = 4
-LAG = 3
+LAG = 4
 
 
 def sketch_kernel(

time: 190 us -> 185 us (0.974)
  Pallas kernels: 188 us -> 183 us
    pallas_call x1, Pallas kernels: 188 us -> 183 us  [whole_call(): pl.pallas_call(functools.partial(whole_kernel, ns, nr, ends), out_shape=(...]
where the time goes in v8:
time: 185 us
  Pallas kernels  183 us (99%)
    pallas_call x1, Pallas kernels, whole_call(): pl.pallas_call(functools.partial(whole_kernel, ns, nr, ends), out_shape=(...  183 us

profile of v8, /device:TPU:1, one launch (start us, length us, event | category | flops | bytes accessed | tf_op | source)
XLA Modules:
  0.0 185.1 jit_solution(7930427811557099705)
XLA Ops:
  0.6 182.6 %shard_map.50 = (f32[4,64]{1,0:T(4,128)}, f32[4,256]{1,0:T(4,128)}) custom-call(bf16[2,256,1024]{2,1,0:T(8,128)(2,1)} %bitcast.1, bf16[1024,256]{1,0:T(8,128)(2,1)} %basis_ref.1, bf16[4,1024]{1,0:T(4,128)(2,1)} %vec_ref.1), custom_call_target="tpu_custom_call" | custom-call | tf_op jit(solution)/shard_map/pallas_call | solution.py:984
  183.3 0.0 copy-start
  183.3 1.2 copy.7
  184.5 0.0 copy-done
  184.5 0.6 copy.8
Async XLA Ops:
  183.3 1.3 copy-start

commit v9 on v8

--- a/solution.py
+++ b/solution.py
@@ -30,6 +30,10 @@
 NN = ((1,), (0,))
 NT = ((1,), (1,))
 TN = ((0,), (0,))
+
+
+def far_first(count):
+    return sorted(range(count), key=lambda k: (-min(k, count - k), k))
 
 
 def remote(src, dst, send, recv, section, row):
@@ -73,7 +77,7 @@
     p = p0_ref[...].reshape(rows, n // 2)[:, :128].T[:8]
     probe[...] = p
     combine(0, packed(dot3(split(p), split(s_ref[...]), NN)), cout, *refs[-4:])
-    for step in range(1, nr):
+    for step in far_first(nr)[:-1]:
         remote(cout, cin.at[r], c_send.at[step], c_recv.at[r], FIRST, lax.rem(r + step, nr)).start()
     cin[pl.ds(r, 1)] = cout[...][None]
 
@@ -136,7 +140,9 @@
         nx = split(next_ref[...])
         iv = split(inv_ref[...])
 
-        hi_ref[...], lo_ref[...] = split(dot3(iv, split(cross_ref[...]), NN))
+        @pl.when(s != FIRST)
+        def _():
+            hi_ref[...], lo_ref[...] = split(dot3(iv, split(cross_ref[...]), NN))
 
         @pl.when(s == FIRST)
         def _():
@@ -161,12 +167,18 @@
             sums[q % 2] = sums[q % 2] + cin[q]
         inner = split(unpacked(jnp.concatenate(sums, axis=1)))
 
-        @pl.when(s != LAST)
-        def _():
-            partial = packed(ahead - dot3(inner, (hi_ref[...], lo_ref[...]), NN))
-            combine(1, partial, cout, dout, din, d_send, d_recv)
-            for q in range(nr):
-                remote(cout, cin.at[r], c_send.at[q], c_recv.at[r], after, q).start()
+        def hand_on(change):
+            combine(1, packed(ahead - change), cout, dout, din, d_send, d_recv)
+            for k in far_first(nr):
+                remote(cout, cin.at[r], c_send.at[k], c_recv.at[r], after, lax.rem(r + k, nr)).start()
+
+        @pl.when(s == FIRST)
+        def _():
+            hand_on(dot3(split(dot3(inner, iv, NN)), split(cross_ref[...]), NN))
+
+        @pl.when((s != FIRST) & (s != LAST))
+        def _():
+            hand_on(dot3(inner, (hi_ref[...], lo_ref[...]), NN))
 
         coef = dot3(inner, iv, NN)
         low_part[...] = jnp.where(odd, coef[:, :n], coef[:, n:])
@@ -178,6 +190,16 @@
             remote(moved, probe, p_send, p_recv, after, r).start()
 
         pass_coef.start()
+
+        @pl.when(s == LAST)
+        def _():
+            m = split(moved[...])
+            sq = dot3(m, m, NT)
+            sout[...] = jnp.concatenate([sq, jnp.zeros((8, 120), F32)], axis=1)
+            for step in range(1, nr):
+                peer = lax.rem(r + step, nr)
+                remote(sout, sin.at[r], s_send.at[step], s_recv.at[r], s, peer).start()
+            sin[pl.ds(r, 1)] = sout[...][None]
 
     @pl.when(off)
     def _():
@@ -198,19 +220,9 @@
 
     @pl.when(s == LAST)
     def _():
-        m = split(moved[...])
-        sq = dot3(m, m, NT)
-        sout[...] = jnp.concatenate([sq, jnp.zeros((8, 120), F32)], axis=1)
-        copies = []
         for step in range(1, nr):
             peer = lax.rem(r + step, nr)
-            cp = remote(sout, sin.at[r], s_send.at[step], s_recv.at[r], s, peer)
-            cp.start()
-            copies.append(cp)
-        sin[pl.ds(r, 1)] = sout[...][None]
-        for step in range(1, nr):
-            peer = lax.rem(r + step, nr)
-            remote(sout, sin.at[peer], s_send.at[step], s_recv.at[peer], s, peer).wait_recv()
+            remote(sout, sin.at[peer], s_send.at[step], s_recv.at[peer], s, peer).wait()
         tot = sin[0]
         for q in range(1, nr):
             tot = tot + sin[q]
@@ -221,7 +233,7 @@
                 cp = remote(bout, bin_, b_send.at[t], b_recv, t, r)
                 cp.start()
                 bcs.append(cp)
-        for cp in copies + bcs:
+        for cp in bcs:
             cp.wait_send()
         bin_[...] = tot
 
@@ -390,7 +402,7 @@
         return remote(red.at[i], full.at[i, where], ag_send.at[i, step], ag_recv.at[i, step], s, peer)
 
     def begin(i):
-        for step in range(1, nr):
+        for step in far_first(nr)[:-1]:
             scatter(i, step).start()
 
     def middle(i):
@@ -400,7 +412,7 @@
         for step in range(1, nr):
             total = total + got[i, step]
         red[i] = total
-        for step in range(1, nr):
+        for step in far_first(nr)[:-1]:
             gather(i, step, True).start()
         full[i, span(r), :] = total
 

time: 185 us -> 179 us (0.968)
  Pallas kernels: 183 us -> 176 us
    pallas_call x1, Pallas kernels: 183 us -> 176 us  [whole_call(): pl.pallas_call(functools.partial(whole_kernel, ns, nr, ends), out_shape=(...]
where the time goes in v9:
time: 179 us
  Pallas kernels  176 us (98%)
  local copies, waits for them, and re-layouts  1.84 us (1%)
    pallas_call x1, Pallas kernels, whole_call(): pl.pallas_call(functools.partial(whole_kernel, ns, nr, ends), out_shape=(...  176 us

profile of v9, /device:TPU:1, one launch (start us, length us, event | category | flops | bytes accessed | tf_op | source)
XLA Modules:
  0.0 178.6 jit_solution(12370705473515752779)
XLA Ops:
  0.6 176.1 %shard_map.50 = (f32[4,64]{1,0:T(4,128)}, f32[4,256]{1,0:T(4,128)}) custom-call(bf16[2,256,1024]{2,1,0:T(8,128)(2,1)} %bitcast.1, bf16[1024,256]{1,0:T(8,128)(2,1)} %basis_ref.1, bf16[4,1024]{1,0:T(4,128)(2,1)} %vec_ref.1), custom_call_target="tpu_custom_call" | custom-call | tf_op jit(solution)/shard_map/pallas_call | solution.py:996
  176.7 0.0 copy-start
  176.7 1.2 copy.7
  178.0 0.0 copy-done
  178.0 0.6 copy.8
Async XLA Ops:
  176.7 1.3 copy-start
